TPU v7x, 32 devices: a whole 2x2x4 slice. The times are simulated.
32 devices in a mesh: gx: 2 (over y), gy: 4 (over z), gz: 4 (over x, core).
Axes of the slice: x: 2, y: 2, z: 4, core: 2. Of those that a mesh axis runs over, the one named last changes fastest.
Arguments:
- conserved: float32 [5, 16, 32, 512], P(None, 'gx', 'gy', 'gz'), may hold values from -3 to 4, as said below
- sigma_guess: float32 [16, 32, 512], P('gx', 'gy', 'gz'), may hold values from -30 to 30
Outputs:
- advanced: float32 [5, 16, 32, 512], P(None, 'gx', 'gy', 'gz')
- sigma_field: float32 [16, 32, 512], P('gx', 'gy', 'gz')
Inputs may be any that keep to these rules, and one draw needn't show every extreme that they name: `conserved`: component 0 (density) lies between 0.5 and 2, components 1 to 3 (momenta) between -3 and 3, component 4 (energy) between 1 and 4.
All inputs are finite; a program needn't handle non-finite values.
Results may differ from a plain program's by a relative error of at most 0.00002.
Values sent between devices are 32-bit elements; how exact they have to be, the bound alone decides.
A program may use at most 64 MiB of HBM per device.

v0:
```python
import functools
import itertools

import jax
import jax.numpy as jnp
from jax import lax
from jax.experimental import pallas as pl
from jax.experimental.pallas import tpu as pltpu
from jax.sharding import PartitionSpec as P

SWEEPS = 4
ALPHA = 10.0
GAMMA = 1.4
LAMBDA = 3.0
STEP_DT = 0.4
MESH = pl.DeviceIdType.MESH
AXES = ("gx", "gy", "gz")

OFFSETS = [o for o in itertools.product((-1, 0, 1), repeat=3) if 1 <= sum(abs(v) for v in o) <= 2]
NEAR = [o for o in OFFSETS if sum(abs(v) for v in o) == 1]
Z_MOVES = [o for o in OFFSETS if o[2] != 0]
XY_MOVES = [o for o in OFFSETS if o[0] != 0 and o[1] != 0]


def neg(offset):
    return tuple(-v for v in offset)


def iota(shape, dim):
    return lax.broadcasted_iota(jnp.int32, shape, dim)


def roll(value, shift, axis):
    size = value.shape[axis]
    shift = shift % size
    return value if shift == 0 else pltpu.roll(value, shift, axis)


def ring(core, ghost, step, axis):
    size = core.shape[axis]
    a, b = roll(core, -step, axis), roll(ghost, -step, axis)
    edge = iota(core.shape, axis) == (size - 1 if step == 1 else 0)
    return jnp.where(edge, b, a), jnp.where(edge, a, b)


def kernel(sizes, cons_hbm, sig_hbm, adv_ref, out_sig_ref, cons, sig,
           yas, zas, xar, xsr, yar, zar,
           ybs, yrs, zrs, xbr, xer, xtr, ybr, yrr, zrr, drr,
           s1, src, y2s, z2s, x2r, x2q, y2r, z2r, d2r,
           s3, y3s, z3s, x3r, y3r, z3r, d3r,
           in_sem, send_sem, recv_sem):
    X, R, L = sig.shape
    me = [lax.axis_index(a) for a in AXES]

    def device(offset):
        return {a: lax.rem(me[i] + offset[i] + sizes[i], sizes[i]) for i, a in enumerate(AXES)}

    load_c = pltpu.make_async_copy(cons_hbm, cons, in_sem.at[0])
    load_s = pltpu.make_async_copy(sig_hbm, sig, in_sem.at[1])
    load_c.start()
    load_s.start()
    barrier = pltpu.get_barrier_semaphore()
    for o in NEAR:
        pl.semaphore_signal(barrier, inc=1, device_id=device(o), device_id_type=MESH)

    sent = []
    count = [0]

    def send(src, dst, offset):
        n = count[0]
        count[0] += 1
        copy = pltpu.make_async_remote_copy(
            src_ref=src, dst_ref=dst, send_sem=send_sem.at[n], recv_sem=recv_sem.at[n],
            device_id=device(offset), device_id_type=MESH)
        copy.start()
        sent.append(copy)
        return copy

    rows = lambda shape: iota(shape, len(shape) - 2)
    lanes = lambda shape: iota(shape, len(shape) - 1)

    def pack_rows(field, first, n):
        size = X * n // R
        out = field[0:size]
        r = rows(out.shape)
        for g in range(1, R // n):
            part = roll(field[g * size:(g + 1) * size], n * g, 1)
            out = jnp.where((r + (2 * R - first - n * g)) % R < n, part, out)
        return out

    def unpack_rows(after, before, n):
        low = rows(after.shape) < R // 2
        return jnp.concatenate(
            [jnp.where(low, roll(after, -n * g, 1), roll(before, -n * g, 1)) for g in range(R // n)], axis=0)

    lane2, row2 = lanes((R, L)), rows((R, L))

    def pack_lanes(fields, width):
        out = jnp.zeros((R, L), jnp.float32)
        for k, tile in enumerate(f[p] for f in fields for p in range(X)):
            out = jnp.where(((lane2 + width // 2) % L) // width == k, roll(tile, width * k, 1), out)
        return out

    def merge_lanes(after, before, width):
        return jnp.where(lanes(after.shape) % width < width // 2, after, before)

    def unpack_lanes(packed, ks, width):
        return jnp.concatenate([roll(packed, -width * k, 1)[None] for k in ks], axis=0)

    def cat(*parts):
        return jnp.concatenate(parts, axis=0)

    def wait(copies):
        for copy in copies:
            copy.wait_recv()

    ups = ((0, 1), (1, -1))

    def edge(d, count, back=0):
        return pl.ds(X - count - back, count) if d == 1 else pl.ds(back, count)

    def send_z(src_ref, dst_ref):
        return [send(src_ref, dst_ref.at[n], o) for n, o in enumerate(Z_MOVES)]

    def z_tiles(buf, e, width, f=0):
        def of(dx, dy):
            return merge_lanes(buf[Z_MOVES.index((-dx, -dy, -1))], buf[Z_MOVES.index((-dx, -dy, 1))], width)
        k = f * X
        z = cat(unpack_lanes(of(-1, 0), range(k + X - e, k + X), width),
                unpack_lanes(of(0, 0), range(k, k + X), width),
                unpack_lanes(of(1, 0), range(k, k + e), width))
        diag = jnp.where(row2 < R // 2, of(0, 1), of(0, -1))
        return z, unpack_lanes(diag, range(k, k + X), width)

    def corners(buf, dx):
        after, before = buf[XY_MOVES.index((-dx, -1, 0))], buf[XY_MOVES.index((-dx, 1, 0))]
        return jnp.where(rows(after.shape) < R // 2, after, before)

    load_c.wait()
    load_s.wait()
    pl.semaphore_wait(barrier, len(NEAR))
    got1 = []
    state = [cons[f] for f in range(4)] + [sig[...]]
    for f in range(5):
        yas[0, f] = pack_rows(state[f], R - 1, 1)
        yas[1, f] = pack_rows(state[f], 0, 1)
    for j, d in ups:
        got1.append(send(yas.at[j], yar.at[j], (0, d, 0)))
    for j, d in ups:
        got1.append(send(cons.at[0:4, edge(d, 1)], xar.at[j], (d, 0, 0)))
        got1.append(send(sig.at[edge(d, 1)], xsr.at[j], (d, 0, 0)))
    energy = cons[4]
    zas[0] = pack_lanes(state[0:4], 4)
    zas[1] = pack_lanes([state[4], energy], 4)
    for j, d in ups:
        got1.append(send(zas, zar.at[j], (0, 0, d)))

    late, late_rho = [], []
    for f in range(4):
        field = state[1 + f] if f < 3 else energy
        ybs[0, f] = pack_rows(field, R - 2, 2)
        ybs[1, f] = pack_rows(field, 0, 2)
    yrs[0] = pack_rows(state[0], R // 2, R // 2)
    yrs[1] = pack_rows(state[0], 0, R // 2)
    for j, d in ups:
        late.append(send(yrs.at[j], yrr.at[j], (0, d, 0)))
        late.append(send(ybs.at[j], ybr.at[j], (0, d, 0)))
        late.append(send(cons.at[0:5, edge(d, 1, 1)], xbr.at[j], (d, 0, 0)))
        late.append(send(cons.at[4, edge(d, 1)], xer.at[j], (d, 0, 0)))
        late_rho.append(send(cons.at[0, edge(d, 1, 2)], xtr.at[j], (d, 0, 0)))
    zrs[...] = pack_lanes([state[0]], 8)

    wait(got1)
    late_rho += [send(cons.at[0, edge(o[0], 2)], drr.at[n], o) for n, o in enumerate(XY_MOVES)]
    late_rho += send_z(zrs, zrr)

    zmerged = [merge_lanes(zar[1, v], zar[0, v], 4) for v in range(2)]

    def near(f):
        ghost_x = (xar[0, f], xar[1, f]) if f < 4 else (xsr[0], xsr[1])
        y = unpack_rows(yar[1, f], yar[0, f], 1)
        z = unpack_lanes(zmerged[f // 4], [(f % 4) * X + p for p in range(X)], 4)
        return cat(ghost_x[0], state[f], ghost_x[1]), y, z

    def neighbours(field):
        c, y, z = field
        m = c[1:X + 1]
        return [(c[2:X + 2], c[0:X]),
                (ring(m, y, 1, 1)[0], ring(m, y, -1, 1)[0]),
                (ring(m, z, 1, 2)[0], ring(m, z, -1, 2)[0])]

    def coefficients(inv_m, inv_n):
        ws = [[0.5 * (inv_m + inv_n[d][s]) for s in range(2)] for d in range(3)]
        return ws, ALPHA / (inv_m + ALPHA * sum(w for pair in ws for w in pair))

    def update(source, ws, scale, nbr):
        acc = source
        for d in range(3):
            for s in range(2):
                acc = acc + ws[d][s] * nbr[d][s]
        return acc * scale

    ext = [near(f) for f in range(5)]
    inv = tuple(1.0 / v for v in ext[0])
    g = []
    for k in (1, 2, 3):
        n = neighbours(tuple(m * r for m, r in zip(ext[k], inv)))
        g.append([0.5 * (n[d][0] - n[d][1]) for d in range(3)])
    div = g[0][0] + g[1][1] + g[2][2]
    source = (g[0][0] * g[0][0] + g[1][1] * g[1][1] + g[2][2] * g[2][2]
              + 2.0 * (g[0][1] * g[1][0] + g[0][2] * g[2][0] + g[1][2] * g[2][1]) + div * div)
    src[...] = source
    near_w, near_scale = coefficients(inv[0][1:X + 1], neighbours(inv))
    sigma1 = update(source, near_w, near_scale, neighbours(ext[4]))

    s1[...] = sigma1
    for j, first in ((0, R - 2), (1, 0)):
        y2s[j, 0] = pack_rows(sigma1, first, 2)
        y2s[j, 1] = pack_rows(source, first, 2)
    z2s[...] = pack_lanes([sigma1, source], 4)
    got2 = [send(s1.at[X - 1 if o[0] == 1 else 0], d2r.at[n], o) for n, o in enumerate(XY_MOVES)]
    got2 += send_z(z2s, z2r)
    for j, d in ups:
        got2.append(send(y2s.at[j], y2r.at[j], (0, d, 0)))
        got2.append(send(s1.at[edge(d, 2)], x2r.at[j], (d, 0, 0)))
        got2.append(send(src.at[edge(d, 2)], x2q.at[j], (d, 0, 0)))

    wait(late)
    core = state[0:4] + [energy]
    rho_y = unpack_rows(yrr[1], yrr[0], R // 2)
    xc = [cat(xbr[0, f], xar[0, f], core[f], xar[1, f], xbr[1, f]) for f in range(4)]
    xc.append(cat(xbr[0, 4], xer[0], energy, xer[1], xbr[1, 4]))
    yc = [rho_y] + [unpack_rows(ybr[1, f], ybr[0, f], 2) for f in range(4)]
    zc = [ext[f][2] for f in range(4)] + [unpack_lanes(zmerged[1], range(X, 2 * X), 4)]

    def x_stencil(c):
        return c[0:X + 1], c[1:X + 2], c[2:X + 3], c[3:X + 4]

    def ring_stencil(c, gh, axis):
        m, p = ring(c, gh, -1, axis), ring(c, gh, 1, axis)
        return cat(*m), cat(c, gh), cat(*p), cat(*ring(p[0], p[1], 1, axis))

    def faces(st):
        m, q, p, pp = st
        sixth = 1.0 / 6.0
        return (5.0 * q + 2.0 * p - m) * sixth, (2.0 * q + 5.0 * p - pp) * sixth

    def plain_flux(s, d):
        r = 1.0 / s[0]
        v = s[1 + d] * r
        pressure = (GAMMA - 1.0) * (s[4] - 0.5 * (s[1] * s[1] + s[2] * s[2] + s[3] * s[3]) * r)
        out = [s[1 + d]]
        for k in range(3):
            out.append(s[1 + k] * v + pressure if k == d else s[1 + k] * v)
        out.append((s[4] + pressure) * v)
        return out, v

    def difference(flux, d):
        if d == 0:
            return flux[1:X + 1] - flux[0:X]
        return flux[0:X] - ring(flux[0:X], flux[X:2 * X], -1, d)[0]

    base = [None] * 5
    speed = []
    for d in range(3):
        if d == 0:
            lr = [faces(x_stencil(c)) for c in xc]
        else:
            lr = [faces(ring_stencil(c, gh, d)) for c, gh in zip(core, (None, yc, zc)[d])]
        lf, lv = plain_flux([v[0] for v in lr], d)
        rf, rv = plain_flux([v[1] for v in lr], d)
        speed.append((lv, rv))
        for k in range(5):
            flux = 0.5 * (lf[k] + rf[k]) - (0.5 * LAMBDA) * (lr[k][1] - lr[k][0])
            change = difference(flux, d)
            base[k] = change if base[k] is None else base[k] + change
    base = [core[k] - STEP_DT * base[k] for k in range(5)]
    adv_ref[0] = base[0]

    def around(field, e):
        c, y, z, w = field
        size = X + 2 * e
        cm = c[1:size + 1]
        own = slice(e, e + X)
        yp, ym = ring(cm, y, 1, 1), ring(cm, y, -1, 1)
        zp, zm = ring(cm, z, 1, 2), ring(cm, z, -1, 2)
        zy = [ring(z[own], w, s, 1)[0] for s in (1, -1)]
        yz = [ring(y[own], w, s, 2)[0] for s in (1, -1)]
        xs = lambda t: (t[e + 1:e + X + 1], t[e - 1:e + X - 1])
        return ([(c[2:size + 2], c[0:size]), (yp[0], ym[0]), (zp[0], zm[0])],
                [xs(y), (yp[1][own], ym[1][own]), yz],
                [xs(z), zy, (zp[1][own], zm[1][own])])

    wait(late_rho)
    rho_c = cat(xtr[0], xc[0], xtr[1])
    rho_z, rho_w = z_tiles(zrr, 2, 8)
    inv = tuple(1.0 / v for v in (rho_c, cat(corners(drr, -1), rho_y, corners(drr, 1)), rho_z, rho_w))
    inv_n = around(inv, 2)
    inv_m = (inv[0][1:X + 5], inv[1][2:X + 2], inv[2][2:X + 2])
    coef = [coefficients(m, n) for m, n in zip(inv_m, inv_n)]

    wait(got2)
    z, w = z_tiles(z2r, 1, 4)
    field = (cat(x2r[0], sigma1, x2r[1]),
             cat(corners(d2r, -1)[None], unpack_rows(y2r[1, 0], y2r[0, 0], 2), corners(d2r, 1)[None]), z, w)
    zs = merge_lanes(z2r[Z_MOVES.index((0, 0, -1))], z2r[Z_MOVES.index((0, 0, 1))], 4)
    sources = (cat(x2q[0], source, x2q[1]), unpack_rows(y2r[1, 1], y2r[0, 1], 2),
               unpack_lanes(zs, range(X, 2 * X), 4))
    inner = slice(1, X + 3)
    n = around(field, 1)
    c = update(sources[0][inner], [[v[inner] for v in pair] for pair in coef[0][0]], coef[0][1][inner], n[0])
    y = update(sources[1], *coef[1], n[1])
    z = update(sources[2], *coef[2], n[2])
    sigma3 = update(source, near_w, near_scale, neighbours((c, y, z)))

    s3[...] = sigma3
    y3s[0] = pack_rows(sigma3, R // 2, R // 2)
    y3s[1] = pack_rows(sigma3, 0, R // 2)
    z3s[...] = pack_lanes([sigma3], 8)
    got3 = [send(s3.at[edge(o[0], 2)], d3r.at[k], o) for k, o in enumerate(XY_MOVES)]
    got3 += send_z(z3s, z3r)
    for j, d in ups:
        got3.append(send(y3s.at[j], y3r.at[j], (0, d, 0)))
        got3.append(send(s3.at[edge(d, 3)], x3r.at[j], (d, 0, 0)))
    wait(got3)

    z, w = z_tiles(z3r, 2, 8)
    field = (cat(x3r[0], sigma3, x3r[1]),
             cat(corners(d3r, -1), unpack_rows(y3r[1], y3r[0], R // 2), corners(d3r, 1)), z, w)
    n = around(field, 2)
    c, y, z = (update(sources[t], *coef[t], n[t]) for t in range(3))
    sigma4 = c[2:X + 2]
    out_sig_ref[...] = sigma4
    total = base[4]
    for d in range(3):
        ls, rs = faces(x_stencil(c) if d == 0 else ring_stencil(sigma4, y if d == 1 else z, d))
        lv, rv = speed[d]
        adv_ref[1 + d] = base[1 + d] - (0.5 * STEP_DT) * difference(ls + rs, d)
        total = total - (0.5 * STEP_DT) * difference(ls * lv + rs * rv, d)
    adv_ref[4] = total
    for copy in sent:
        copy.wait_send()


def solution(mesh):
    sizes = tuple(mesh.shape[a] for a in AXES)

    def on_device(conserved, sigma_guess):
        X, R, L = sigma_guess.shape
        A, B, H = X // R, 2 * X // R, X // 2
        f32 = jnp.float32
        vm = lambda *shape: pltpu.VMEM(shape, f32)
        nz, nd = len(Z_MOVES), len(XY_MOVES)
        messages = 80
        return pl.pallas_call(
            functools.partial(kernel, sizes),
            out_shape=(pltpu.VMEM(conserved.shape, f32), pltpu.VMEM(sigma_guess.shape, f32)),
            in_specs=[pl.BlockSpec(memory_space=pl.ANY)] * 2,
            out_specs=(pl.BlockSpec(memory_space=pltpu.VMEM),) * 2,
            scratch_shapes=[
                vm(*conserved.shape), vm(X, R, L),
                vm(2, 5, A, R, L), vm(2, R, L), vm(2, 4, 1, R, L), vm(2, 1, R, L), vm(2, 5, A, R, L), vm(2, 2, R, L),
                vm(2, 4, B, R, L), vm(2, H, R, L), vm(R, L), vm(2, 5, 1, R, L), vm(2, 1, R, L), vm(2, 1, R, L),
                vm(2, 4, B, R, L), vm(2, H, R, L), vm(nz, R, L), vm(nd, 2, R, L),
                vm(X, R, L), vm(X, R, L), vm(2, 2, B, R, L), vm(R, L),
                vm(2, 2, R, L), vm(2, 2, R, L), vm(2, 2, B, R, L), vm(nz, R, L), vm(nd, R, L),
                vm(X, R, L), vm(2, H, R, L), vm(R, L),
                vm(2, 3, R, L), vm(2, H, R, L), vm(nz, R, L), vm(nd, 2, R, L),
                pltpu.SemaphoreType.DMA((2,)),
                pltpu.SemaphoreType.DMA((messages,)),
                pltpu.SemaphoreType.DMA((messages,)),
            ],
            compiler_params=pltpu.CompilerParams(collective_id=0, has_side_effects=True),
        )(conserved, sigma_guess)

    specs = (P(None, "gx", "gy", "gz"), P("gx", "gy", "gz"))
    return jax.shard_map(on_device, mesh=mesh, in_specs=specs, out_specs=specs, check_vma=False)
```

profile of v0, /device:TPU:0, one launch (start us, length us, event | category | flops | bytes accessed | tf_op | source)
XLA Modules:
  0.0 22.8 jit_solution(9630169368355717244)
XLA Ops:
  0.6 20.9 %shard_map.41 = (f32[5,8,8,128]{3,2,1,0:T(8,128)S(1)}, f32[8,8,128]{2,1,0:T(8,128)S(1)}) custom-call(f32[5,8,8,128]{3,2,1,0:T(8,128)} %cons_hbm.1, f32[8,8,128]{2,1,0:T(8,128)} %sig_hbm.1), custom_call_target="tpu_custom_call" | custom-call | tf_op jit(solution)/shard_map/pallas_call | solution.py:355
  21.5 0.7 %copy.6 = f32[5,8,8,128]{3,2,1,0:T(8,128)} copy(f32[5,8,8,128]{3,2,1,0:T(8,128)S(1)} %get-tuple-element.2) | data formatting | bytes 327680
  22.2 0.6 %copy.7 = f32[8,8,128]{2,1,0:T(8,128)} copy(f32[8,8,128]{2,1,0:T(8,128)S(1)} %get-tuple-element.3) | data formatting | bytes 65536
where the time goes:
time: 22.9 us; the launch traced here: 22.8 us
  Pallas kernels  20.9 us (91%)
  local copies, waits for them, and re-layouts  1.28 us (6%)
  between operations  0.64 us (3%)
    pallas_call x1, Pallas kernels, on_device(): pl.pallas_call(functools.partial(kernel, sizes), out_shape=(pltpu.VMEM(co...  20.9 us
    unnamed x2, local copies, waits for them, and re-layouts  1.28 us

commit v1 on v0

v1 whole, which is shorter than its diff:
```python
import functools
import itertools

import jax
import jax.numpy as jnp
from jax import lax
from jax.experimental import pallas as pl
from jax.experimental.pallas import tpu as pltpu
from jax.sharding import PartitionSpec as P

SWEEPS = 4
ALPHA = 10.0
GAMMA = 1.4
LAMBDA = 3.0
STEP_DT = 0.4
DEPTH = SWEEPS
MESH = pl.DeviceIdType.MESH
AXES = ("gx", "gy", "gz")

OFFSETS = [o for o in itertools.product((-1, 0, 1), repeat=3) if any(o)]
NEAR = [o for o in OFFSETS if sum(abs(v) for v in o) == 1]
XY_MOVES = [o for o in OFFSETS if o[0] != 0 and o[1] != 0 and o[2] == 0]
Z_NEAR = [(0, 0, 1), (0, 0, -1)]
Z_VERTEX = [o for o in OFFSETS if all(o)]
Z_EDGE = [o for o in OFFSETS if o[2] != 0 and o not in Z_NEAR and o not in Z_VERTEX]


def iota(shape, dim):
    return lax.broadcasted_iota(jnp.int32, shape, dim)


def roll(value, shift, axis):
    size = value.shape[axis]
    shift = shift % size
    return value if shift == 0 else pltpu.roll(value, shift, axis)


def ring(core, ghost, step, axis):
    size = core.shape[axis]
    a, b = roll(core, -step, axis), roll(ghost, -step, axis)
    edge = iota(core.shape, axis) == (size - 1 if step == 1 else 0)
    return jnp.where(edge, b, a), jnp.where(edge, a, b)


def distinct(moves, sizes):
    first = {}
    return {o: first.setdefault(tuple(v % s for v, s in zip(o, sizes)), o) for o in moves}


def landing(X, R, sizes):
    count = lambda moves: len(set(distinct(moves, sizes).values()))
    A, B, H = X // R, 2 * X // R, X // 2
    return [
        2 * (5 * A + 5 + 2),
        2 * (H + A + 4 * B + 5 + 1 + DEPTH - 1),
        count(Z_NEAR),
        2 * len(XY_MOVES) + count(Z_EDGE) + count(Z_VERTEX),
        2 * len(XY_MOVES) + count(Z_NEAR) + count(Z_EDGE) + count(Z_VERTEX) + 2 * 2 * H + 2 * 2 * DEPTH,
    ]


def kernel(sizes, cons_hbm, sig_hbm, adv_ref, out_sig_ref, cons, sig, g0, g1, g2, g3, g4,
           yas, zas, ybs, yrs, zrs, drs, x2s, y2s, z2s, d2s, in_sem, ready, send_sem, recv_sem):
    X, R, L = sig.shape
    H, D, DZ = R // 2, DEPTH, L // (4 * X)
    me = [lax.axis_index(a) for a in AXES]

    def device(offset):
        return {a: lax.rem(me[i] + offset[i] + sizes[i], sizes[i]) for i, a in enumerate(AXES)}

    load_c = pltpu.make_async_copy(cons_hbm, cons, in_sem.at[0])
    load_s = pltpu.make_async_copy(sig_hbm, sig, in_sem.at[1])
    load_c.start()
    load_s.start()
    barrier = pltpu.get_barrier_semaphore()
    for o in NEAR:
        pl.semaphore_signal(barrier, inc=1, device_id=device(o), device_id_type=MESH)

    class Group:
        def __init__(self, n, buf):
            self.n, self.buf, self.used = n, buf, 0

        def copy(self, src, dst, offset):
            return pltpu.make_async_remote_copy(
                src_ref=src, dst_ref=dst, send_sem=send_sem.at[self.n], recv_sem=recv_sem.at[self.n],
                device_id=device(offset), device_id_type=MESH)

        def send(self, src, offset):
            at = self.used
            if len(src.shape) == 2:
                self.used += 1
                self.copy(src, self.buf.at[at], offset).start()
            else:
                self.used += src.shape[0]
                self.copy(src, self.buf.at[at:self.used], offset).start()
            return at

        def arrived(self):
            assert self.used == self.buf.shape[0]
            self.copy(self.buf, self.buf, NEAR[0]).wait_recv()

        def left(self):
            self.copy(self.buf, self.buf, NEAR[0]).wait_send()

    groups = [Group(n, buf) for n, buf in enumerate((g0, g1, g2, g3, g4))]
    first, late, side, late_rho, second = groups

    rows = lambda shape: iota(shape, len(shape) - 2)
    lanes = lambda shape: iota(shape, len(shape) - 1)

    def pack_rows(field, first, n):
        size = X * n // R
        out = field[0:size]
        r = rows(out.shape)
        for g in range(1, R // n):
            part = roll(field[g * size:(g + 1) * size], n * g, 1)
            out = jnp.where((r + (2 * R - first - n * g)) % R < n, part, out)
        return out

    def unpack_rows(after, before, n, reach=0):
        low = rows(after.shape) < H
        return jnp.concatenate(
            [jnp.where(low, roll(after, -n * g - reach, 1), roll(before, reach - n * g, 1)) for g in range(R // n)],
            axis=0)

    lane2, row2 = lanes((R, L)), rows((R, L))
    low2 = row2 < H

    def pack_lanes(fields, width):
        out = jnp.zeros((R, L), jnp.float32)
        for k, tile in enumerate(f[p] for f in fields for p in range(X)):
            out = jnp.where(((lane2 + width // 2) % L) // width == k, roll(tile, width * k, 1), out)
        return out

    def merge_lanes(after, before, width):
        return jnp.where(lanes(after.shape) % width < width // 2, after, before)

    def unpack_lanes(packed, ks, width):
        return [roll(packed, -width * k, 1)[None] for k in ks]

    def pack_corner(f, s, o):
        a1, a2, a3, a4 = (f[X - a if o[0] == 1 else a - 1] for a in range(1, 5))
        if o[1] == 1:
            one = jnp.where(row2 >= H, a1, jnp.where(row2 >= 1, roll(a2, -H, 0), roll(a4, 1, 0)))
            two = roll(a3, 2, 0)
        else:
            one = jnp.where(row2 < H, a1, jnp.where(row2 < R - 1, roll(a2, H, 0), roll(a4, -1, 0)))
            two = roll(a3, -2, 0)
        if s is not None:
            s1, s2, s3 = (s[X - a if o[0] == 1 else a - 1] for a in range(1, 4))
            if o[1] == 1:
                two = jnp.where(row2 > H, s1, jnp.where(row2 == H, roll(s3, 1 - H, 0),
                                                        jnp.where(row2 >= 2, roll(s2, -H, 0), two)))
            else:
                two = jnp.where(row2 < H - 1, s1, jnp.where(row2 == H - 1, roll(s3, H - 1, 0),
                                                            jnp.where(row2 < R - 2, roll(s2, H, 0), two)))
        return one, two

    def unpack_corner(buf, slots, dx, source):
        after, before = slots[(-dx, -1, 0)], slots[(-dx, 1, 0)]
        fa, fb, sa, sb = buf[after], buf[before], buf[after + 1], buf[before + 1]
        if source:
            out = [jnp.where(low2, sa, sb), roll(jnp.where(low2, sb, sa), H, 0),
                   jnp.where(low2, roll(sa, 1 - H, 0), roll(sb, H - 1, 0))]
        else:
            out = [jnp.where(low2, fa, fb), roll(jnp.where(low2, fb, fa), H, 0),
                   jnp.where(low2, roll(sa, 2, 0), roll(sb, -2, 0)),
                   jnp.where(low2, roll(fa, 1, 0), roll(fb, -1, 0))]
        out = [v[None] for v in out]
        return out if dx == 1 else out[::-1]

    def cat(*parts):
        return jnp.concatenate(parts, axis=0)

    ups = ((0, 1), (1, -1))

    def plane(d, back=0):
        return X - 1 - back if d == 1 else back

    def planes(d, count, back=0):
        return slice(X - count - back, X - back) if d == 1 else slice(back, back + count)

    def send_z(group, src_ref, moves, slots):
        for o, same in distinct(moves, sizes).items():
            slots[o] = group.send(src_ref, o) if o == same else slots[same]

    def z_tiles(buf, slots, e, ew, width, f=0):
        def of(dx, dy):
            return merge_lanes(buf[slots[(-dx, -dy, -1)]], buf[slots[(-dx, -dy, 1)]], width)

        def diag(dx):
            return jnp.where(low2, of(dx, 1), of(dx, -1))

        k = f * X
        spread = lambda t, e: cat(*unpack_lanes(t(-1), range(k + X - e, k + X), width),
                                  *unpack_lanes(t(0), range(k, k + X), width),
                                  *unpack_lanes(t(1), range(k, k + e), width))
        return spread(lambda dx: of(dx, 0), e), spread(diag, ew)

    load_c.wait()
    load_s.wait()
    pl.semaphore_wait(barrier, len(NEAR))
    state = [cons[f] for f in range(4)] + [sig[...]]
    A, B = X // R, 2 * X // R
    for f in range(5):
        yas[0, f * A:(f + 1) * A] = pack_rows(state[f], R - 1, 1)
        yas[1, f * A:(f + 1) * A] = pack_rows(state[f], 0, 1)
    ya = [first.send(yas.at[j], (0, d, 0)) for j, d in ups]
    xa = []
    for j, d in ups:
        xa.append(first.send(cons.at[0:4, plane(d)], (d, 0, 0)))
        first.send(sig.at[plane(d)], (d, 0, 0))
    energy = cons[4]
    zas[0] = pack_lanes(state[0:4], 4)
    zas[1] = pack_lanes([state[4], energy], 4)
    za = [first.send(zas, (0, 0, d)) for j, d in ups]
    for o in NEAR:
        pl.semaphore_signal(ready, inc=1, device_id=device(o), device_id_type=MESH)

    for f in range(4):
        field = state[1 + f] if f < 3 else energy
        ybs[0, f * B:(f + 1) * B] = pack_rows(field, R - 2, 2)
        ybs[1, f * B:(f + 1) * B] = pack_rows(field, 0, 2)
    for j, start, beyond in ((0, H, H - 1), (1, 0, H)):
        yrs[j, 0:X // 2] = pack_rows(state[0], start, H)
        yrs[j, X // 2:X // 2 + A] = pack_rows(state[0], beyond, 1)
    yr, yb, xb, xe, xt = [], [], [], [], []
    for j, d in ups:
        yr.append(late.send(yrs.at[j], (0, d, 0)))
        yb.append(late.send(ybs.at[j], (0, d, 0)))
        xb.append(late.send(cons.at[0:5, plane(d, 1)], (d, 0, 0)))
        xe.append(late.send(cons.at[4, plane(d)], (d, 0, 0)))
        xt.append(late.send(cons.at[0, planes(d, D - 1, 2)], (d, 0, 0)))
    zrs[...] = pack_lanes([state[0]], 4 * DZ)
    for n, o in enumerate(XY_MOVES):
        drs[n, 0], drs[n, 1] = pack_corner(state[0], None, o)

    pl.semaphore_wait(ready, len(NEAR))
    zr, dr = {}, {}
    send_z(side, zrs, Z_NEAR, zr)
    side_slots = dict(zr)
    for n, o in enumerate(XY_MOVES):
        dr[o] = late_rho.send(drs.at[n], o)
    zr_far = {}
    send_z(late_rho, zrs, Z_EDGE, zr_far)
    side.arrived()
    send_z(late_rho, zrs, Z_VERTEX, zr_far)

    first.arrived()
    zmerged = [merge_lanes(g0[za[1] + v], g0[za[0] + v], 4) for v in range(2)]

    def near(f):
        y = unpack_rows(g0[ya[1] + f * A:ya[1] + (f + 1) * A], g0[ya[0] + f * A:ya[0] + (f + 1) * A], 1)
        z = cat(*unpack_lanes(zmerged[f // 4], [(f % 4) * X + p for p in range(X)], 4))
        return cat(g0[xa[0] + f][None], state[f], g0[xa[1] + f][None]), y, z

    def neighbours(field):
        c, y, z = field
        m = c[1:X + 1]
        return [(c[2:X + 2], c[0:X]),
                (ring(m, y, 1, 1)[0], ring(m, y, -1, 1)[0]),
                (ring(m, z, 1, 2)[0], ring(m, z, -1, 2)[0])]

    def coefficients(inv_m, inv_n):
        ws = [[0.5 * (inv_m + inv_n[d][s]) for s in range(2)] for d in range(3)]
        return ws, ALPHA / (inv_m + ALPHA * sum(w for pair in ws for w in pair))

    def update(source, ws, scale, nbr):
        acc = source
        for d in range(3):
            for s in range(2):
                acc = acc + ws[d][s] * nbr[d][s]
        return acc * scale

    ext = [near(f) for f in range(5)]
    inv = tuple(1.0 / v for v in ext[0])
    g = []
    for k in (1, 2, 3):
        n = neighbours(tuple(m * r for m, r in zip(ext[k], inv)))
        g.append([0.5 * (n[d][0] - n[d][1]) for d in range(3)])
    div = g[0][0] + g[1][1] + g[2][2]
    source = (g[0][0] * g[0][0] + g[1][1] * g[1][1] + g[2][2] * g[2][2]
              + 2.0 * (g[0][1] * g[1][0] + g[0][2] * g[2][0] + g[1][2] * g[2][1]) + div * div)
    near_w, near_scale = coefficients(inv[0][1:X + 1], neighbours(inv))
    sigma1 = update(source, near_w, near_scale, neighbours(ext[4]))

    z_fold = jnp.where(lanes(source.shape) == DZ - 1, near_w[2][0] * roll(sigma1, -1, 2),
                       jnp.where(lanes(source.shape) == L - DZ, near_w[2][1] * roll(sigma1, 1, 2), 0.0))
    z2s[...] = pack_lanes([sigma1, source + z_fold], 2 * DZ)
    z2, d2 = {}, {}
    send_z(second, z2s, Z_VERTEX, z2)
    for n, o in enumerate(XY_MOVES):
        d2s[n, 0], d2s[n, 1] = pack_corner(sigma1, source, o)
        d2[o] = second.send(d2s.at[n], o)
    send_z(second, z2s, Z_EDGE, z2)
    y_fold = jnp.where(rows(source.shape) == H - 1, near_w[1][0] * roll(sigma1, -1, 1),
                       jnp.where(rows(source.shape) == H, near_w[1][1] * roll(sigma1, 1, 1), 0.0))
    for j, start in ((0, H), (1, 0)):
        y2s[j, 0:X // 2] = pack_rows(sigma1, start, H)
        y2s[j, X // 2:X] = pack_rows(source + y_fold, start, H)
    y2 = [second.send(y2s.at[j], (0, d, 0)) for j, d in ups]
    for j, d in ups:
        x2s[j, 0:D] = sigma1[planes(d, D)]
        x2s[j, D:2 * D] = source[planes(d, D)]
    x2s[0, D] = source[X - D] + near_w[0][1][X - D] * sigma1[X - D - 1]
    x2s[1, 2 * D - 1] = source[D - 1] + near_w[0][0][D - 1] * sigma1[D]
    x2 = [second.send(x2s.at[j], (d, 0, 0)) for j, d in ups]
    send_z(second, z2s, Z_NEAR, z2)

    late.arrived()
    core = state[0:4] + [energy]
    rho_y = unpack_rows(g1[yr[1]:yr[1] + X // 2], g1[yr[0]:yr[0] + X // 2], H)
    rho_yy = unpack_rows(g1[yr[1] + X // 2:yr[1] + X // 2 + A], g1[yr[0] + X // 2:yr[0] + X // 2 + A], 1, 1)
    xn = [[g0[xa[j] + f][None] for f in range(4)] + [g1[xe[j]][None]] for j in range(2)]
    xc = [cat(g1[xb[0] + f][None], xn[0][f], core[f], xn[1][f], g1[xb[1] + f][None]) for f in range(5)]
    yc = [rho_y] + [unpack_rows(g1[yb[1] + f * B:yb[1] + (f + 1) * B], g1[yb[0] + f * B:yb[0] + (f + 1) * B], 2)
                    for f in range(4)]
    zc = [ext[f][2] for f in range(4)] + [cat(*unpack_lanes(zmerged[1], range(X, 2 * X), 4))]

    def x_stencil(c):
        return c[0:X + 1], c[1:X + 2], c[2:X + 3], c[3:X + 4]

    def ring_stencil(c, gh, axis):
        m, p = ring(c, gh, -1, axis), ring(c, gh, 1, axis)
        return cat(*m), cat(c, gh), cat(*p), cat(*ring(p[0], p[1], 1, axis))

    def faces(st):
        m, q, p, pp = st
        sixth = 1.0 / 6.0
        return (5.0 * q + 2.0 * p - m) * sixth, (2.0 * q + 5.0 * p - pp) * sixth

    def plain_flux(s, d):
        r = 1.0 / s[0]
        v = s[1 + d] * r
        pressure = (GAMMA - 1.0) * (s[4] - 0.5 * (s[1] * s[1] + s[2] * s[2] + s[3] * s[3]) * r)
        out = [s[1 + d]]
        for k in range(3):
            out.append(s[1 + k] * v + pressure if k == d else s[1 + k] * v)
        out.append((s[4] + pressure) * v)
        return out, v

    def difference(flux, d):
        if d == 0:
            return flux[1:X + 1] - flux[0:X]
        return flux[0:X] - ring(flux[0:X], flux[X:2 * X], -1, d)[0]

    base = [None] * 5
    speed = []
    for d in range(3):
        if d == 0:
            lr = [faces(x_stencil(c)) for c in xc]
        else:
            lr = [faces(ring_stencil(c, gh, d)) for c, gh in zip(core, (None, yc, zc)[d])]
        lf, lv = plain_flux([v[0] for v in lr], d)
        rf, rv = plain_flux([v[1] for v in lr], d)
        speed.append((lv, rv))
        for k in range(5):
            flux = 0.5 * (lf[k] + rf[k]) - (0.5 * LAMBDA) * (lr[k][1] - lr[k][0])
            change = difference(flux, d)
            base[k] = change if base[k] is None else base[k] + change
    base = [core[k] - STEP_DT * base[k] for k in range(5)]
    adv_ref[0] = base[0]

    def cut(part, e, step=0):
        value, reach = part
        return value[reach - e + step:reach + X + e + step]

    def around(field, reach, beyond=None):
        c, y, z, w = field
        ec, ey, ez, ew = reach
        inner = lambda t, e, to: t[e - to:e + X + to]
        cy = [ring(cut(c, ec), cut(y, ec), s, 1) for s in (1, -1)]
        cz = [ring(cut(c, ec), cut(z, ec), s, 2) for s in (1, -1)]
        zy = [ring(cut(z, ez), cut(w, ez), s, 1) for s in (1, -1)]
        yz = [ring(cut(y, ey), cut(w, ey), s, 2) for s in (1, -1)]
        yy = [inner(t[1], ec, ey) for t in cy]
        if beyond is not None:
            yy = [jnp.where(rows(t.shape) == at, beyond, t) for t, at in zip(yy, (H - 1, H))]
        xs = lambda part, e: (cut(part, e, 1), cut(part, e, -1))
        out = [[xs(c, ec), [t[0] for t in cy], [t[0] for t in cz]],
               [xs(y, ey), yy, [t[0] for t in yz]],
               [xs(z, ez), [t[0] for t in zy], [inner(t[1], ec, ez) for t in cz]]]
        if ew is not None:
            out.append([xs(w, ew), [inner(t[1], ez, ew) for t in zy], [inner(t[1], ey, ew) for t in yz]])
        return out

    late_rho.arrived()
    reach = (D, D - 1, D - 1, D - 2)
    rho_c = cat(g1[xt[0]:xt[0] + D - 1], xc[0], g1[xt[1]:xt[1] + D - 1])
    rho_ye = cat(*unpack_corner(g3, dr, -1, False), rho_y, *unpack_corner(g3, dr, 1, False))
    rho_buf = {o: g2[at] for o, at in side_slots.items()}
    rho_buf.update({o: g3[at] for o, at in zr_far.items()})
    rho_z, rho_w = z_tiles(rho_buf, {o: o for o in rho_buf}, D, D - 1, 4 * DZ)
    inv = [1.0 / v for v in (rho_c, rho_ye, rho_z, rho_w)]
    inv = tuple(zip(inv, (D + 1, D, D, D - 1)))
    edge = jnp.zeros((D - 1, R, L), jnp.float32)
    inv_n = around(inv, reach, cat(edge, 1.0 / rho_yy, edge))
    coef = [coefficients(cut(m, e), n) for m, e, n in zip(inv, reach, inv_n)]

    def mute(t, axis):
        size = t[0].shape[axis]
        depth = H if axis == 1 else DZ
        at = iota(t[0].shape, axis)
        return [jnp.where(at == depth - 1, 0.0, t[0]), jnp.where(at == size - depth, 0.0, t[1])]

    coef[1][0][1] = mute(coef[1][0][1], 1)
    coef[2][0][2] = mute(coef[2][0][2], 2)

    second.arrived()
    zero = jnp.zeros((1, R, L), jnp.float32)
    sig_z, sig_w = z_tiles(g4, z2, D, D - 1, 2 * DZ)
    src_z, src_w = z_tiles(g4, z2, D - 1, D - 2, 2 * DZ, 1)
    y_own = [unpack_rows(g4[y2[1] + t:y2[1] + t + X // 2], g4[y2[0] + t:y2[0] + t + X // 2], H) for t in (0, X // 2)]
    field = ((cat(zero, g4[x2[0]:x2[0] + D], sigma1, g4[x2[1]:x2[1] + D], zero), D + 1),
             (cat(*unpack_corner(g4, d2, -1, False), y_own[0], *unpack_corner(g4, d2, 1, False)), D),
             (sig_z, D), (sig_w, D - 1))
    sources = [cat(g4[x2[0] + D:x2[0] + 2 * D], source, g4[x2[1] + D:x2[1] + 2 * D]),
               cat(*unpack_corner(g4, d2, -1, True), y_own[1], *unpack_corner(g4, d2, 1, True)), src_z, src_w]
    have = reach
    for sweep in range(1, SWEEPS):
        last = sweep == SWEEPS - 1
        to = (2, 0, 0, None) if last else tuple(e - sweep + 1 for e in reach)
        nbr = around(field, to)
        out = []
        for t, n in enumerate(nbr):
            s = lambda v: cut((v, have[t]), to[t])
            ws, scale = coef[t]
            out.append(update(s(sources[t]), [[s(v) for v in pair] for pair in ws], s(scale), n))
        field = tuple(zip(out, to))

    c, y, z = (v for v, _ in field)
    sigma4 = c[2:X + 2]
    out_sig_ref[...] = sigma4
    total = base[4]
    for d in range(3):
        ls, rs = faces(x_stencil(c) if d == 0 else ring_stencil(sigma4, y if d == 1 else z, d))
        lv, rv = speed[d]
        adv_ref[1 + d] = base[1 + d] - (0.5 * STEP_DT) * difference(ls + rs, d)
        total = total - (0.5 * STEP_DT) * difference(ls * lv + rs * rv, d)
    adv_ref[4] = total
    for group in groups:
        group.left()


def solution(mesh):
    sizes = tuple(mesh.shape[a] for a in AXES)

    def on_device(conserved, sigma_guess):
        X, R, L = sigma_guess.shape
        A, B, H, D = X // R, 2 * X // R, X // 2, DEPTH
        f32 = jnp.float32
        vm = lambda *shape: pltpu.VMEM((*shape, R, L), f32)
        nd = len(XY_MOVES)
        tiles = landing(X, R, sizes)
        return pl.pallas_call(
            functools.partial(kernel, sizes),
            out_shape=(pltpu.VMEM(conserved.shape, f32), pltpu.VMEM(sigma_guess.shape, f32)),
            in_specs=[pl.BlockSpec(memory_space=pl.ANY)] * 2,
            out_specs=(pl.BlockSpec(memory_space=pltpu.VMEM),) * 2,
            scratch_shapes=[
                vm(5, X), vm(X), *[vm(n) for n in tiles],
                vm(2, 5 * A), vm(2), vm(2, 4 * B), vm(2, H + A), vm(), vm(nd, 2),
                vm(2, 2 * D), vm(2, 2 * H), vm(), vm(nd, 2),
                pltpu.SemaphoreType.DMA((2,)),
                pltpu.SemaphoreType.REGULAR,
                pltpu.SemaphoreType.DMA((len(tiles),)),
                pltpu.SemaphoreType.DMA((len(tiles),)),
            ],
            compiler_params=pltpu.CompilerParams(collective_id=0, has_side_effects=True),
        )(conserved, sigma_guess)

    specs = (P(None, "gx", "gy", "gz"), P("gx", "gy", "gz"))
    return jax.shard_map(on_device, mesh=mesh, in_specs=specs, out_specs=specs, check_vma=False)
```

time: 22.9 us -> 18.3 us (0.80)
  Pallas kernels: 20.9 us -> 16.3 us
    pallas_call x1, Pallas kernels: 20.9 us -> 16.3 us  [on_device(): pl.pallas_call(functools.partial(kernel, sizes), out_shape=(pltpu.VMEM(co...]
where the time goes in v1:
time: 18.3 us; the launch traced here: 18.2 us
  Pallas kernels  16.3 us (89%)
  local copies, waits for them, and re-layouts  1.28 us (7%)
  between operations  0.64 us (3%)
    pallas_call x1, Pallas kernels, on_device(): pl.pallas_call(functools.partial(kernel, sizes), out_shape=(pltpu.VMEM(co...  16.3 us
    unnamed x2, local copies, waits for them, and re-layouts  1.28 us

profile of v1, /device:TPU:0, one launch (start us, length us, event | category | flops | bytes accessed | tf_op | source)
XLA Modules:
  0.0 18.2 jit_solution(7054716828560487834)
XLA Ops:
  0.6 16.3 %shard_map.41 = (f32[5,8,8,128]{3,2,1,0:T(8,128)S(1)}, f32[8,8,128]{2,1,0:T(8,128)S(1)}) custom-call(f32[5,8,8,128]{3,2,1,0:T(8,128)} %cons_hbm.1, f32[8,8,128]{2,1,0:T(8,128)} %sig_hbm.1), custom_call_target="tpu_custom_call" | custom-call | tf_op jit(solution)/shard_map/pallas_call | solution.py:455
  16.9 0.7 %copy.6 = f32[5,8,8,128]{3,2,1,0:T(8,128)} copy(f32[5,8,8,128]{3,2,1,0:T(8,128)S(1)} %get-tuple-element.2) | data formatting | bytes 327680
  17.6 0.6 %copy.7 = f32[8,8,128]{2,1,0:T(8,128)} copy(f32[8,8,128]{2,1,0:T(8,128)S(1)} %get-tuple-element.3) | data formatting | bytes 65536

commit v2 on v1

--- a/solution.py
+++ b/solution.py
@@ -18,7 +18,7 @@
 AXES = ("gx", "gy", "gz")
 
 OFFSETS = [o for o in itertools.product((-1, 0, 1), repeat=3) if any(o)]
-NEAR = [o for o in OFFSETS if sum(abs(v) for v in o) == 1]
+NEAR = [(0, 1, 0), (0, -1, 0), (1, 0, 0), (-1, 0, 0), (0, 0, 1), (0, 0, -1)]
 XY_MOVES = [o for o in OFFSETS if o[0] != 0 and o[1] != 0 and o[2] == 0]
 Z_NEAR = [(0, 0, 1), (0, 0, -1)]
 Z_VERTEX = [o for o in OFFSETS if all(o)]
@@ -199,20 +199,20 @@
 
     load_c.wait()
     load_s.wait()
-    pl.semaphore_wait(barrier, len(NEAR))
     state = [cons[f] for f in range(4)] + [sig[...]]
+    energy = cons[4]
     A, B = X // R, 2 * X // R
     for f in range(5):
         yas[0, f * A:(f + 1) * A] = pack_rows(state[f], R - 1, 1)
         yas[1, f * A:(f + 1) * A] = pack_rows(state[f], 0, 1)
+    zas[0] = pack_lanes(state[0:4], 4)
+    zas[1] = pack_lanes([state[4], energy], 4)
+    pl.semaphore_wait(barrier, len(NEAR))
     ya = [first.send(yas.at[j], (0, d, 0)) for j, d in ups]
     xa = []
     for j, d in ups:
         xa.append(first.send(cons.at[0:4, plane(d)], (d, 0, 0)))
         first.send(sig.at[plane(d)], (d, 0, 0))
-    energy = cons[4]
-    zas[0] = pack_lanes(state[0:4], 4)
-    zas[1] = pack_lanes([state[4], energy], 4)
     za = [first.send(zas, (0, 0, d)) for j, d in ups]
     for o in NEAR:
         pl.semaphore_signal(ready, inc=1, device_id=device(o), device_id_type=MESH)
@@ -442,6 +442,15 @@
         group.left()
 
 
+def write(adv, sig, adv_hbm, sig_hbm, sem):
+    copies = [pltpu.make_async_copy(src, dst, sem.at[n])
+              for n, (src, dst) in enumerate(((adv, adv_hbm), (sig, sig_hbm)))]
+    for copy in copies:
+        copy.start()
+    for copy in copies:
+        copy.wait()
+
+
 def solution(mesh):
     sizes = tuple(mesh.shape[a] for a in AXES)
 
@@ -452,7 +461,7 @@
         vm = lambda *shape: pltpu.VMEM((*shape, R, L), f32)
         nd = len(XY_MOVES)
         tiles = landing(X, R, sizes)
-        return pl.pallas_call(
+        outs = pl.pallas_call(
             functools.partial(kernel, sizes),
             out_shape=(pltpu.VMEM(conserved.shape, f32), pltpu.VMEM(sigma_guess.shape, f32)),
             in_specs=[pl.BlockSpec(memory_space=pl.ANY)] * 2,
@@ -468,6 +477,13 @@
             ],
             compiler_params=pltpu.CompilerParams(collective_id=0, has_side_effects=True),
         )(conserved, sigma_guess)
+        return pl.pallas_call(
+            write,
+            out_shape=tuple(jax.ShapeDtypeStruct(a.shape, f32) for a in (conserved, sigma_guess)),
+            in_specs=[pl.BlockSpec(memory_space=pltpu.VMEM)] * 2,
+            out_specs=(pl.BlockSpec(memory_space=pl.ANY),) * 2,
+            scratch_shapes=[pltpu.SemaphoreType.DMA((2,))],
+        )(*(pltpu.with_memory_space_constraint(v, pltpu.VMEM) for v in outs))
 
     specs = (P(None, "gx", "gy", "gz"), P("gx", "gy", "gz"))
     return jax.shard_map(on_device, mesh=mesh, in_specs=specs, out_specs=specs, check_vma=False)

time: 18.3 us -> 17.8 us (0.973)
  local copies, waits for them, and re-layouts: 1.28 us -> 0 us
  Pallas kernels: 16.3 us -> 17 us
    unnamed x2 -> x0, local copies, waits for them, and re-layouts: 1.28 us -> none
    pallas_call x0 -> x1, Pallas kernels: none -> 0.69 us  [on_device(): pl.pallas_call(write, out_shape=tuple((jax.ShapeDtypeStruct(a.shape, f32)...]
where the time goes in v2:
time: 17.8 us; the launch traced here: 17.7 us
  Pallas kernels  17 us (96%)
  between operations  0.64 us (4%)
    pallas_call x1, Pallas kernels, on_device(): pl.pallas_call(functools.partial(kernel, sizes), out_shape=(pltpu.VMEM(co...  16.4 us
    pallas_call x1, Pallas kernels, on_device(): pl.pallas_call(write, out_shape=tuple((jax.ShapeDtypeStruct(a.shape, f32)...  0.69 us

profile of v2, /device:TPU:0, one launch (start us, length us, event | category | flops | bytes accessed | tf_op | source)
XLA Modules:
  0.0 17.7 jit_solution(15246321341257121008)
XLA Ops:
  0.6 16.4 %shard_map.41 = (f32[5,8,8,128]{3,2,1,0:T(8,128)S(1)}, f32[8,8,128]{2,1,0:T(8,128)S(1)}) custom-call(f32[5,8,8,128]{3,2,1,0:T(8,128)} %cons_hbm.1, f32[8,8,128]{2,1,0:T(8,128)} %sig_hbm.1), custom_call_target="tpu_custom_call" | custom-call | tf_op jit(solution)/shard_map/pallas_call | solution.py:464
  17.0 0.7 %shard_map.42 = (f32[5,8,8,128]{3,2,1,0:T(8,128)}, f32[8,8,128]{2,1,0:T(8,128)}) custom-call(f32[5,8,8,128]{3,2,1,0:T(8,128)S(1)} %get-tuple-element.4.adv, f32[8,8,128]{2,1,0:T(8,128)S(1)} %get-tuple-element.5.sig), custom_call_target="tpu_custom_call" | custom-call | tf_op jit(solution)/shard_map/pallas_call | solution.py:480

commit v3 on v2

--- a/solution.py
+++ b/solution.py
@@ -63,6 +63,7 @@
            yas, zas, ybs, yrs, zrs, drs, x2s, y2s, z2s, d2s, in_sem, ready, send_sem, recv_sem):
     X, R, L = sig.shape
     H, D, DZ = R // 2, DEPTH, L // (4 * X)
+    wide = 2 * DZ
     me = [lax.axis_index(a) for a in AXES]
 
     def device(offset):
@@ -132,11 +133,13 @@
             out = jnp.where(((lane2 + width // 2) % L) // width == k, roll(tile, width * k, 1), out)
         return out
 
-    def merge_lanes(after, before, width):
-        return jnp.where(lanes(after.shape) % width < width // 2, after, before)
-
-    def unpack_lanes(packed, ks, width):
-        return [roll(packed, -width * k, 1)[None] for k in ks]
+    slot2 = ((lane2 + DZ) % L) // wide
+    side2 = lane2 % wide >= DZ
+
+    def pack_planes(out, value, ps):
+        for k, p in enumerate(ps):
+            out = jnp.where(slot2 == p % (2 * X), roll(value[k], wide * p, 1), out)
+        return out
 
     def pack_corner(f, s, o):
         a1, a2, a3, a4 = (f[X - a if o[0] == 1 else a - 1] for a in range(1, 5))
@@ -184,18 +187,19 @@
         for o, same in distinct(moves, sizes).items():
             slots[o] = group.send(src_ref, o) if o == same else slots[same]
 
-    def z_tiles(buf, slots, e, ew, width, f=0):
-        def of(dx, dy):
-            return merge_lanes(buf[slots[(-dx, -dy, -1)]], buf[slots[(-dx, -dy, 1)]], width)
-
-        def diag(dx):
-            return jnp.where(low2, of(dx, 1), of(dx, -1))
-
-        k = f * X
-        spread = lambda t, e: cat(*unpack_lanes(t(-1), range(k + X - e, k + X), width),
-                                  *unpack_lanes(t(0), range(k, k + X), width),
-                                  *unpack_lanes(t(1), range(k, k + e), width))
-        return spread(lambda dx: of(dx, 0), e), spread(diag, ew)
+    def z_side(of, dy, dz, f):
+        own, after, before = (of(dx, dy, dz) for dx in (0, 1, -1))
+        if f == 0:
+            return jnp.where(slot2 < X, own, roll(jnp.where(slot2 < X // 2, after, before), L // 2, 1))
+        return jnp.where(slot2 < X, roll(own, L // 2, 1), jnp.where(slot2 < X + X // 2, after, before))
+
+    def sides(own, low, high):
+        return jnp.where(side2, low, own), jnp.where(side2, own, high)
+
+    def z_pairs(of, f, own_z, own_w):
+        z = [z_side(of, 0, dz, f) for dz in (-1, 1)]
+        w = [jnp.where(low2, z_side(of, 1, dz, f), z_side(of, -1, dz, f)) for dz in (-1, 1)]
+        return sides(own_z, *z), sides(own_w, *w)
 
     load_c.wait()
     load_s.wait()
@@ -231,7 +235,11 @@
         xb.append(late.send(cons.at[0:5, plane(d, 1)], (d, 0, 0)))
         xe.append(late.send(cons.at[4, plane(d)], (d, 0, 0)))
         xt.append(late.send(cons.at[0, planes(d, D - 1, 2)], (d, 0, 0)))
-    zrs[...] = pack_lanes([state[0]], 4 * DZ)
+    lane3 = lanes(energy.shape)
+    row3 = rows(energy.shape)
+    rho_zz = jnp.where(lane3 == DZ - 1, roll(state[0], -1, 2), roll(state[0], 1, 2))
+    rho_own = pack_lanes([state[0], rho_zz], wide)
+    zrs[...] = rho_own
     for n, o in enumerate(XY_MOVES):
         drs[n, 0], drs[n, 1] = pack_corner(state[0], None, o)
 
@@ -246,55 +254,71 @@
     side.arrived()
     send_z(late_rho, zrs, Z_VERTEX, zr_far)
 
+    inv0 = 1.0 / state[0]
+    fields = [inv0] + [state[k] * inv0 for k in (1, 2, 3)] + [state[4]]
+    own = [[[roll(v, -s, axis) for s in (1, -1)] for axis in (1, 2)] for v in fields]
+    region = ((lane2 + 2) % L) // (4 * X)
+
     first.arrived()
-    zmerged = [merge_lanes(g0[za[1] + v], g0[za[0] + v], 4) for v in range(2)]
-
-    def near(f):
-        y = unpack_rows(g0[ya[1] + f * A:ya[1] + (f + 1) * A], g0[ya[0] + f * A:ya[0] + (f + 1) * A], 1)
-        z = cat(*unpack_lanes(zmerged[f // 4], [(f % 4) * X + p for p in range(X)], 4))
-        return cat(g0[xa[0] + f][None], state[f], g0[xa[1] + f][None]), y, z
-
-    def neighbours(field):
-        c, y, z = field
-        m = c[1:X + 1]
-        return [(c[2:X + 2], c[0:X]),
-                (ring(m, y, 1, 1)[0], ring(m, y, -1, 1)[0]),
-                (ring(m, z, 1, 2)[0], ring(m, z, -1, 2)[0])]
+
+    def to_speed(t):
+        r = 1.0 / t[0]
+        return [r] + [m * r for m in t[1:4]] + [t[4]]
+
+    xg = [to_speed([g0[xa[j] + f] for f in range(5)]) for j in range(2)]
+    yg = [to_speed([g0[ya[j] + f * A:ya[j] + (f + 1) * A] for f in range(5)]) for j in range(2)]
+    zmerged = [jnp.where(lane2 % 4 < 2, g0[za[1] + v], g0[za[0] + v]) for v in range(2)]
+    zinv = 1.0 / jnp.where(region == 0, zmerged[0], 1.0)
+    shifted = [roll(zinv, 4 * X * k, 1) for k in (1, 2, 3)]
+    zspeed = zmerged[0] * jnp.where(region == 1, shifted[0], jnp.where(region == 2, shifted[1], shifted[2]))
+    zspeed = jnp.where(region == 0, zinv, zspeed)
+
+    def neighbours(f):
+        v, ((yp, ym), (zp, zm)) = fields[f], own[f]
+        after = cat(*[roll(yg[1][f], R - 1 - p, 1) for p in range(R)])
+        before = cat(*[roll(yg[0][f], 1 - p, 1) for p in range(R)])
+        t, k = (zspeed, f * X) if f < 4 else (zmerged[1], 0)
+        high = cat(*[roll(t, L - 1 - 4 * (k + p), 1)[None] for p in range(X)])
+        low = cat(*[roll(t, 1 - 4 * (k + p), 1)[None] for p in range(X)])
+        return [(cat(v[1:X], xg[1][f][None]), cat(xg[0][f][None], v[0:X - 1])),
+                (jnp.where(row3 == R - 1, after, yp), jnp.where(row3 == 0, before, ym)),
+                (jnp.where(lane3 == L - 1, high, zp), jnp.where(lane3 == 0, low, zm))]
 
     def coefficients(inv_m, inv_n):
-        ws = [[0.5 * (inv_m + inv_n[d][s]) for s in range(2)] for d in range(3)]
-        return ws, ALPHA / (inv_m + ALPHA * sum(w for pair in ws for w in pair))
-
-    def update(source, ws, scale, nbr):
+        ws = [[inv_m + inv_n[d][s] for s in range(2)] for d in range(3)]
+        scale = ALPHA / (2.0 * inv_m + ALPHA * sum(w for pair in ws for w in pair))
+        return [[w * scale for w in pair] for pair in ws], scale
+
+    def update(source, ws, nbr):
         acc = source
         for d in range(3):
             for s in range(2):
                 acc = acc + ws[d][s] * nbr[d][s]
-        return acc * scale
-
-    ext = [near(f) for f in range(5)]
-    inv = tuple(1.0 / v for v in ext[0])
+        return acc
+
+    near_w, near_scale = coefficients(inv0, neighbours(0))
     g = []
     for k in (1, 2, 3):
-        n = neighbours(tuple(m * r for m, r in zip(ext[k], inv)))
-        g.append([0.5 * (n[d][0] - n[d][1]) for d in range(3)])
+        n = neighbours(k)
+        g.append([n[d][0] - n[d][1] for d in range(3)])
     div = g[0][0] + g[1][1] + g[2][2]
     source = (g[0][0] * g[0][0] + g[1][1] * g[1][1] + g[2][2] * g[2][2]
               + 2.0 * (g[0][1] * g[1][0] + g[0][2] * g[2][0] + g[1][2] * g[2][1]) + div * div)
-    near_w, near_scale = coefficients(inv[0][1:X + 1], neighbours(inv))
-    sigma1 = update(source, near_w, near_scale, neighbours(ext[4]))
-
-    z_fold = jnp.where(lanes(source.shape) == DZ - 1, near_w[2][0] * roll(sigma1, -1, 2),
-                       jnp.where(lanes(source.shape) == L - DZ, near_w[2][1] * roll(sigma1, 1, 2), 0.0))
-    z2s[...] = pack_lanes([sigma1, source + z_fold], 2 * DZ)
+    source = source * (0.5 * near_scale)
+    sigma1 = update(source, near_w, neighbours(4))
+
+    z_fold = jnp.where(lane3 == DZ - 1, near_w[2][0] * roll(sigma1, -1, 2),
+                       jnp.where(lane3 == L - DZ, near_w[2][1] * roll(sigma1, 1, 2), 0.0))
+    z_own = pack_lanes([sigma1, source + z_fold], wide)
+    z2s[...] = z_own
     z2, d2 = {}, {}
     send_z(second, z2s, Z_VERTEX, z2)
     for n, o in enumerate(XY_MOVES):
         d2s[n, 0], d2s[n, 1] = pack_corner(sigma1, source, o)
         d2[o] = second.send(d2s.at[n], o)
     send_z(second, z2s, Z_EDGE, z2)
-    y_fold = jnp.where(rows(source.shape) == H - 1, near_w[1][0] * roll(sigma1, -1, 1),
-                       jnp.where(rows(source.shape) == H, near_w[1][1] * roll(sigma1, 1, 1), 0.0))
+    y_fold = jnp.where(row3 == H - 1, near_w[1][0] * roll(sigma1, -1, 1),
+                       jnp.where(row3 == H, near_w[1][1] * roll(sigma1, 1, 1), 0.0))
     for j, start in ((0, H), (1, 0)):
         y2s[j, 0:X // 2] = pack_rows(sigma1, start, H)
         y2s[j, X // 2:X] = pack_rows(source + y_fold, start, H)
@@ -315,7 +339,8 @@
     xc = [cat(g1[xb[0] + f][None], xn[0][f], core[f], xn[1][f], g1[xb[1] + f][None]) for f in range(5)]
     yc = [rho_y] + [unpack_rows(g1[yb[1] + f * B:yb[1] + (f + 1) * B], g1[yb[0] + f * B:yb[0] + (f + 1) * B], 2)
                     for f in range(4)]
-    zc = [ext[f][2] for f in range(4)] + [cat(*unpack_lanes(zmerged[1], range(X, 2 * X), 4))]
+    zc = [cat(*[roll(zmerged[f // 4], -4 * (f * X + p), 1)[None] for p in range(X)]) for f in range(4)]
+    zc.append(cat(*[roll(zmerged[1], -4 * (X + p), 1)[None] for p in range(X)]))
 
     def x_stencil(c):
         return c[0:X + 1], c[1:X + 2], c[2:X + 3], c[3:X + 4]
@@ -361,82 +386,127 @@
     base = [core[k] - STEP_DT * base[k] for k in range(5)]
     adv_ref[0] = base[0]
 
-    def cut(part, e, step=0):
+    def lower(v, d):
+        return v[0:X] if d == 0 else ring(v[0:X], v[X:2 * X], -1, d)[0]
+
+    part = []
+    for d, (lv, rv) in enumerate(speed):
+        ll, rl = lower(lv, d), lower(rv, d)
+        lv, rv = (lv[1:X + 1], rv[1:X + 1]) if d == 0 else (lv[0:X], rv[0:X])
+        k = -0.5 * STEP_DT / 6.0
+        part.append([k * ll, k * (-lv - 5.0 * ll - 2.0 * rl), k * (5.0 * lv + 2.0 * rv - 2.0 * ll - 5.0 * rl),
+                     k * (2.0 * lv + 5.0 * rv + rl), -k * rv])
+    middle = part[0][2] + part[1][2] + part[2][2]
+
+    def pick(part, ps, step=0):
         value, reach = part
-        return value[reach - e + step:reach + X + e + step]
-
-    def around(field, reach, beyond=None):
-        c, y, z, w = field
-        ec, ey, ez, ew = reach
-        inner = lambda t, e, to: t[e - to:e + X + to]
-        cy = [ring(cut(c, ec), cut(y, ec), s, 1) for s in (1, -1)]
-        cz = [ring(cut(c, ec), cut(z, ec), s, 2) for s in (1, -1)]
-        zy = [ring(cut(z, ez), cut(w, ez), s, 1) for s in (1, -1)]
-        yz = [ring(cut(y, ey), cut(w, ey), s, 2) for s in (1, -1)]
-        yy = [inner(t[1], ec, ey) for t in cy]
-        if beyond is not None:
-            yy = [jnp.where(rows(t.shape) == at, beyond, t) for t, at in zip(yy, (H - 1, H))]
-        xs = lambda part, e: (cut(part, e, 1), cut(part, e, -1))
-        out = [[xs(c, ec), [t[0] for t in cy], [t[0] for t in cz]],
-               [xs(y, ey), yy, [t[0] for t in yz]],
-               [xs(z, ez), [t[0] for t in zy], [inner(t[1], ec, ez) for t in cz]]]
-        if ew is not None:
-            out.append([xs(w, ew), [inner(t[1], ez, ew) for t in zy], [inner(t[1], ey, ew) for t in yz]])
+        return cat(*[value[reach + a + step:reach + b + step] for a, b in ps])
+
+    def z_shift(value, ps, pair, step, by=1):
+        at = [p for a, b in ps for p in range(a, b)]
+        lane = lanes(value.shape)
+        if step == 1:
+            ghost, edge = [roll(pair[1], L - by - wide * p, 1) for p in at], lane >= L - by
+        else:
+            ghost, edge = [roll(pair[0], by - wide * p, 1) for p in at], lane < by
+        return jnp.where(edge, cat(*[v[None] for v in ghost]), roll(value, -step * by, 2))
+
+    def around_planes(c, y, pair, ps):
+        m = pick(c, ps)
+        cy = [ring(m, pick(y, ps), s, 1) for s in (1, -1)]
+        z = [z_shift(m, ps, pair, s) for s in (1, -1)]
+        return [(pick(c, ps, 1), pick(c, ps, -1)), [t[0] for t in cy], z], [t[1] for t in cy]
+
+    def around_ghosts(y, yy, pair, e):
+        ps = [(-e, X + e)]
+        return [(pick(y, ps, 1), pick(y, ps, -1)), yy, [z_shift(pick(y, ps), ps, pair, s) for s in (1, -1)]]
+
+    def around_packed(z, w):
+        out = [], []
+        for zt, wt in zip(z, w):
+            zy = [ring(zt, wt, s, 0) for s in (1, -1)]
+            for to, t, k in ((out[0], zt, 0), (out[1], wt, 1)):
+                to.append([(roll(t, -wide, 1), roll(t, wide, 1)), [v[k] for v in zy], (roll(t, -1, 1), roll(t, 1, 1))])
         return out
 
     late_rho.arrived()
-    reach = (D, D - 1, D - 1, D - 2)
+    rho_of = lambda dx, dy, dz: g2[side_slots[(0, 0, -dz)]] if dx == dy == 0 else g3[zr_far[(-dx, -dy, -dz)]]
+    every = range(-D, X + D)
+    outer = [p for p in every if not 0 <= p < X]
     rho_c = cat(g1[xt[0]:xt[0] + D - 1], xc[0], g1[xt[1]:xt[1] + D - 1])
     rho_ye = cat(*unpack_corner(g3, dr, -1, False), rho_y, *unpack_corner(g3, dr, 1, False))
-    rho_buf = {o: g2[at] for o, at in side_slots.items()}
-    rho_buf.update({o: g3[at] for o, at in zr_far.items()})
-    rho_z, rho_w = z_tiles(rho_buf, {o: o for o in rho_buf}, D, D - 1, 4 * DZ)
-    inv = [1.0 / v for v in (rho_c, rho_ye, rho_z, rho_w)]
-    inv = tuple(zip(inv, (D + 1, D, D, D - 1)))
-    edge = jnp.zeros((D - 1, R, L), jnp.float32)
-    inv_n = around(inv, reach, cat(edge, 1.0 / rho_yy, edge))
-    coef = [coefficients(cut(m, e), n) for m, e, n in zip(inv, reach, inv_n)]
-
-    def mute(t, axis):
-        size = t[0].shape[axis]
-        depth = H if axis == 1 else DZ
-        at = iota(t[0].shape, axis)
-        return [jnp.where(at == depth - 1, 0.0, t[0]), jnp.where(at == size - depth, 0.0, t[1])]
-
-    coef[1][0][1] = mute(coef[1][0][1], 1)
-    coef[2][0][2] = mute(coef[2][0][2], 2)
+    rho_z, rho_w = z_pairs(rho_of, 0, pack_planes(rho_own, pick((rho_c, D + 1), [(-D, 0), (X, X + D)]), outer),
+                           pack_planes(rho_own, rho_ye, every))
+    inv_c, inv_y = (1.0 / rho_c, D + 1), (1.0 / rho_ye, D)
+    inv_z, inv_w = [1.0 / t for t in rho_z], [1.0 / t for t in rho_w]
+    beyond = [1.0 / z_side(rho_of, 0, dz, 1) for dz in (-1, 1)]
+    far_coef = coefficients(pick(inv_c, [(-D, 0), (X, X + D)]),
+                            around_planes(inv_c, inv_y, inv_z, [(-D, 0), (X, X + D)])[0])[0]
+    coef_c = [[cat(far[0:D], mine, far[D:2 * D]) for far, mine in zip(*pair)] for pair in zip(far_coef, near_w)]
+    e = D - 1
+    rim = jnp.zeros((e, R, L), jnp.float32)
+    yy = around_planes(inv_c, inv_y, inv_z, [(-e, X + e)])[1]
+    inv_yy = cat(rim, 1.0 / rho_yy, rim)
+    row = rows(inv_yy.shape)
+    yy = [jnp.where(row == at, inv_yy, t) for t, at in zip(yy, (H - 1, H))]
+    coef_y = coefficients(pick(inv_y, [(-e, X + e)]), around_ghosts(inv_y, yy, inv_w, e))[0]
+    coef_y[1] = [jnp.where(row == at, 0.0, t) for t, at in zip(coef_y[1], (H - 1, H))]
+    zn, wn = around_packed(inv_z, inv_w)
+    coef_z, coef_w = [], []
+    for j, at in ((0, DZ), (1, DZ - 1)):
+        last = lane2 % wide == at
+        pair = list(zn[j][2])
+        pair[1 - j] = jnp.where(last, beyond[j], pair[1 - j])
+        ws = coefficients(inv_z[j], [*zn[j][0:2], pair])[0]
+        ws[2][1 - j] = jnp.where(last, 0.0, ws[2][1 - j])
+        coef_z.append(ws)
+        coef_w.append(coefficients(inv_w[j], wn[j])[0])
 
     second.arrived()
     zero = jnp.zeros((1, R, L), jnp.float32)
-    sig_z, sig_w = z_tiles(g4, z2, D, D - 1, 2 * DZ)
-    src_z, src_w = z_tiles(g4, z2, D - 1, D - 2, 2 * DZ, 1)
-    y_own = [unpack_rows(g4[y2[1] + t:y2[1] + t + X // 2], g4[y2[0] + t:y2[0] + t + X // 2], H) for t in (0, X // 2)]
-    field = ((cat(zero, g4[x2[0]:x2[0] + D], sigma1, g4[x2[1]:x2[1] + D], zero), D + 1),
-             (cat(*unpack_corner(g4, d2, -1, False), y_own[0], *unpack_corner(g4, d2, 1, False)), D),
-             (sig_z, D), (sig_w, D - 1))
-    sources = [cat(g4[x2[0] + D:x2[0] + 2 * D], source, g4[x2[1] + D:x2[1] + 2 * D]),
-               cat(*unpack_corner(g4, d2, -1, True), y_own[1], *unpack_corner(g4, d2, 1, True)), src_z, src_w]
-    have = reach
+    sig_of = lambda dx, dy, dz: g4[z2[(-dx, -dy, -dz)]]
+    sx, qx = [cat(g4[x2[0] + t:x2[0] + t + D], g4[x2[1] + t:x2[1] + t + D]) for t in (0, D)]
+    sy, qy = [unpack_rows(g4[y2[1] + t:y2[1] + t + X // 2], g4[y2[0] + t:y2[0] + t + X // 2], H) for t in (0, X // 2)]
+    sy = cat(*unpack_corner(g4, d2, -1, False), sy, *unpack_corner(g4, d2, 1, False))
+    qy = cat(*unpack_corner(g4, d2, -1, True), qy, *unpack_corner(g4, d2, 1, True))
+    z, w = z_pairs(sig_of, 0, pack_planes(z_own, sx, outer), pack_planes(z_own, sy, every))
+    q_own = roll(z_own, L // 2, 1)
+    qz, qw = z_pairs(sig_of, 1, pack_planes(q_own, qx, outer), pack_planes(q_own, qy, range(-e, X + e)))
+    c, y = (cat(zero, sx[0:D], sigma1, sx[D:2 * D], zero), D + 1), (sy, D)
+    qc = cat(qx[0:D], source, qx[D:2 * D])
     for sweep in range(1, SWEEPS):
         last = sweep == SWEEPS - 1
-        to = (2, 0, 0, None) if last else tuple(e - sweep + 1 for e in reach)
-        nbr = around(field, to)
-        out = []
-        for t, n in enumerate(nbr):
-            s = lambda v: cut((v, have[t]), to[t])
-            ws, scale = coef[t]
-            out.append(update(s(sources[t]), [[s(v) for v in pair] for pair in ws], s(scale), n))
-        field = tuple(zip(out, to))
-
-    c, y, z = (v for v, _ in field)
-    sigma4 = c[2:X + 2]
+        ec, ey = D + 1 - sweep, 0 if last else D - sweep
+        cn, yy = around_planes(c, y, z, [(-ec, X + ec)])
+        yn = around_ghosts(y, [t[ec - ey:ec + X + ey] for t in yy], w, ey)
+        zn, wn = around_packed(z, w)
+        cut = lambda v, have, e: v[have - e:have + X + e]
+        c = update(cut(qc, D, ec), [[cut(v, D, ec) for v in pair] for pair in coef_c], cn), ec
+        y = update(cut(qy, D - 1, ey), [[cut(v, D - 1, ey) for v in pair] for pair in coef_y], yn), ey
+        z = [update(qz[j], coef_z[j], zn[j]) for j in range(2)]
+        if not last:
+            w = [update(qw[j], coef_w[j], wn[j]) for j in range(2)]
+
+    own_planes = [(0, X)]
+    sigma4 = pick(c, own_planes)
     out_sig_ref[...] = sigma4
-    total = base[4]
+
+    def y_shift(step, by):
+        edge = row3 >= R - by if step == 1 else row3 < by
+        return jnp.where(edge, roll(y[0], -step * by, 1), roll(sigma4, -step * by, 1))
+
+    total = base[4] + middle * sigma4
     for d in range(3):
-        ls, rs = faces(x_stencil(c) if d == 0 else ring_stencil(sigma4, y if d == 1 else z, d))
-        lv, rv = speed[d]
-        adv_ref[1 + d] = base[1 + d] - (0.5 * STEP_DT) * difference(ls + rs, d)
-        total = total - (0.5 * STEP_DT) * difference(ls * lv + rs * rv, d)
+        if d == 0:
+            near_far = [[pick(c, own_planes, s * by) for by in (1, 2)] for s in (1, -1)]
+        elif d == 1:
+            near_far = [[y_shift(s, by) for by in (1, 2)] for s in (1, -1)]
+        else:
+            near_far = [[z_shift(sigma4, own_planes, z, s, by) for by in (1, 2)] for s in (1, -1)]
+        (p1, p2), (m1, m2) = near_far
+        adv_ref[1 + d] = base[1 + d] + ((-4.0 * STEP_DT / 6.0) * (p1 - m1) + (0.5 * STEP_DT / 6.0) * (p2 - m2))
+        a = part[d]
+        total = total + (a[0] * m2 + a[1] * m1 + a[3] * p1 + a[4] * p2)
     adv_ref[4] = total
     for group in groups:
         group.left()

time: 17.8 us -> 17.6 us (0.989)
  Pallas kernels: 17 us -> 16.8 us
    pallas_call x1, Pallas kernels: 16.4 us -> 16.1 us  [on_device(): pl.pallas_call(functools.partial(kernel, sizes), out_shape=(pltpu.VMEM(co...]
where the time goes in v3:
time: 17.6 us; the launch traced here: 17.4 us
  Pallas kernels  16.8 us (95%)
  between operations  0.64 us (4%)
    pallas_call x1, Pallas kernels, on_device(): pl.pallas_call(functools.partial(kernel, sizes), out_shape=(pltpu.VMEM(co...  16.1 us
    pallas_call x1, Pallas kernels, on_device(): pl.pallas_call(write, out_shape=tuple((jax.ShapeDtypeStruct(a.shape, f32)...  0.69 us

profile of v3, /device:TPU:0, one launch (start us, length us, event | category | flops | bytes accessed | tf_op | source)
XLA Modules:
  0.0 17.4 jit_solution(3415934924694187394)
XLA Ops:
  0.6 16.1 %shard_map.41 = (f32[5,8,8,128]{3,2,1,0:T(8,128)S(1)}, f32[8,8,128]{2,1,0:T(8,128)S(1)}) custom-call(f32[5,8,8,128]{3,2,1,0:T(8,128)} %cons_hbm.1, f32[8,8,128]{2,1,0:T(8,128)} %sig_hbm.1), custom_call_target="tpu_custom_call" | custom-call | tf_op jit(solution)/shard_map/pallas_call | solution.py:534
  16.7 0.7 %shard_map.42 = (f32[5,8,8,128]{3,2,1,0:T(8,128)}, f32[8,8,128]{2,1,0:T(8,128)}) custom-call(f32[5,8,8,128]{3,2,1,0:T(8,128)S(1)} %get-tuple-element.4.adv, f32[8,8,128]{2,1,0:T(8,128)S(1)} %get-tuple-element.5.sig), custom_call_target="tpu_custom_call" | custom-call | tf_op jit(solution)/shard_map/pallas_call | solution.py:550

commit v4 on v3

--- a/solution.py
+++ b/solution.py
@@ -47,19 +47,28 @@
     return {o: first.setdefault(tuple(v % s for v, s in zip(o, sizes)), o) for o in moves}
 
 
+def z_rows(offset, R):
+    n = R if offset[1] == 0 else DEPTH - 1 if offset[0] else DEPTH
+    return slice(0, n) if offset[1] == -1 else slice(R - n, R)
+
+
 def landing(X, R, sizes):
-    count = lambda moves: len(set(distinct(moves, sizes).values()))
+    sent = lambda moves: sorted(set(distinct(moves, sizes).values()))
+    rows = [z_rows(o, R).stop - z_rows(o, R).start for o in sent(Z_EDGE) + sent(Z_VERTEX)]
+    part = [n for n in rows if n < R]
+    full = len(rows) - len(part)
     A, B, H = X // R, 2 * X // R, X // 2
+    near, corner = len(sent(Z_NEAR)), 2 * len(XY_MOVES)
     return [
-        2 * (5 * A + 5 + 2),
-        2 * (H + A + 4 * B + 5 + 1 + DEPTH - 1),
-        count(Z_NEAR),
-        2 * len(XY_MOVES) + count(Z_EDGE) + count(Z_VERTEX),
-        2 * len(XY_MOVES) + count(Z_NEAR) + count(Z_EDGE) + count(Z_VERTEX) + 2 * 2 * H + 2 * 2 * DEPTH,
+        (2 * (5 * A + 5 + 2), []),
+        (2 * (H + A + 4 * B + 5 + 1 + DEPTH - 1), []),
+        (near, []),
+        (corner + full, part),
+        (corner + near + full + 2 * 2 * H + 2 * 2 * DEPTH, part),
     ]
 
 
-def kernel(sizes, cons_hbm, sig_hbm, adv_ref, out_sig_ref, cons, sig, g0, g1, g2, g3, g4,
+def kernel(sizes, cons_hbm, sig_hbm, adv_ref, out_sig_ref, cons, sig, g0, g1, g2, g3, g4, t3, t4,
            yas, zas, ybs, yrs, zrs, drs, x2s, y2s, z2s, d2s, in_sem, ready, send_sem, recv_sem):
     X, R, L = sig.shape
     H, D, DZ = R // 2, DEPTH, L // (4 * X)
@@ -78,32 +87,39 @@
         pl.semaphore_signal(barrier, inc=1, device_id=device(o), device_id_type=MESH)
 
     class Group:
-        def __init__(self, n, buf):
-            self.n, self.buf, self.used = n, buf, 0
+        def __init__(self, n, buf, spare):
+            self.n, self.buf, self.spare, self.used, self.rows = n, buf, spare, 0, 0
 
         def copy(self, src, dst, offset):
             return pltpu.make_async_remote_copy(
                 src_ref=src, dst_ref=dst, send_sem=send_sem.at[self.n], recv_sem=recv_sem.at[self.n],
                 device_id=device(offset), device_id_type=MESH)
 
-        def send(self, src, offset):
+        def send(self, src, offset, part=None):
             at = self.used
-            if len(src.shape) == 2:
+            if part is not None:
                 self.used += 1
+                self.rows += part.stop - part.start
+                self.copy(src.at[part], self.buf.at[at, part], offset).start()
+            elif len(src.shape) == 2:
+                self.used, self.rows = at + 1, self.rows + R
                 self.copy(src, self.buf.at[at], offset).start()
             else:
-                self.used += src.shape[0]
+                self.used, self.rows = at + src.shape[0], self.rows + R * src.shape[0]
                 self.copy(src, self.buf.at[at:self.used], offset).start()
             return at
 
+        def whole(self):
+            assert self.used == self.buf.shape[0] and self.rows == self.spare.shape[0] * self.spare.shape[1]
+            return self.copy(self.spare, self.spare, NEAR[0])
+
         def arrived(self):
-            assert self.used == self.buf.shape[0]
-            self.copy(self.buf, self.buf, NEAR[0]).wait_recv()
+            self.whole().wait_recv()
 
         def left(self):
-            self.copy(self.buf, self.buf, NEAR[0]).wait_send()
-
-    groups = [Group(n, buf) for n, buf in enumerate((g0, g1, g2, g3, g4))]
+            self.whole().wait_send()
+
+    groups = [Group(n, buf, size) for n, (buf, size) in enumerate(zip((g0, g1, g2, g3, g4), (g0, g1, g2, t3, t4)))]
     first, late, side, late_rho, second = groups
 
     rows = lambda shape: iota(shape, len(shape) - 2)
@@ -185,7 +201,7 @@
 
     def send_z(group, src_ref, moves, slots):
         for o, same in distinct(moves, sizes).items():
-            slots[o] = group.send(src_ref, o) if o == same else slots[same]
+            slots[o] = group.send(src_ref, o, z_rows(o, R)) if o == same else slots[same]
 
     def z_side(of, dy, dz, f):
         own, after, before = (of(dx, dy, dz) for dx in (0, 1, -1))
@@ -531,13 +547,14 @@
         vm = lambda *shape: pltpu.VMEM((*shape, R, L), f32)
         nd = len(XY_MOVES)
         tiles = landing(X, R, sizes)
+        spare = [pltpu.VMEM((R * n + sum(part), 1, L), f32) for n, part in tiles[3:]]
         outs = pl.pallas_call(
             functools.partial(kernel, sizes),
             out_shape=(pltpu.VMEM(conserved.shape, f32), pltpu.VMEM(sigma_guess.shape, f32)),
             in_specs=[pl.BlockSpec(memory_space=pl.ANY)] * 2,
             out_specs=(pl.BlockSpec(memory_space=pltpu.VMEM),) * 2,
             scratch_shapes=[
-                vm(5, X), vm(X), *[vm(n) for n in tiles],
+                vm(5, X), vm(X), *[vm(n + len(part)) for n, part in tiles], *spare,
                 vm(2, 5 * A), vm(2), vm(2, 4 * B), vm(2, H + A), vm(), vm(nd, 2),
                 vm(2, 2 * D), vm(2, 2 * H), vm(), vm(nd, 2),
                 pltpu.SemaphoreType.DMA((2,)),

time: 17.6 us -> 17.2 us (0.977)
  Pallas kernels: 16.8 us -> 16.5 us
    pallas_call x1, Pallas kernels: 16.1 us -> 15.8 us  [on_device(): pl.pallas_call(functools.partial(kernel, sizes), out_shape=(pltpu.VMEM(co...]
where the time goes in v4:
time: 17.2 us; the launch traced here: 17.1 us
  Pallas kernels  16.5 us (96%)
  between operations  0.64 us (4%)
    pallas_call x1, Pallas kernels, on_device(): pl.pallas_call(functools.partial(kernel, sizes), out_shape=(pltpu.VMEM(co...  15.8 us
    pallas_call x1, Pallas kernels, on_device(): pl.pallas_call(write, out_shape=tuple((jax.ShapeDtypeStruct(a.shape, f32)...  0.69 us

profile of v4, /device:TPU:0, one launch (start us, length us, event | category | flops | bytes accessed | tf_op | source)
XLA Modules:
  0.0 17.1 jit_solution(15100231983027036387)
XLA Ops:
  0.6 15.8 %shard_map.41 = (f32[5,8,8,128]{3,2,1,0:T(8,128)S(1)}, f32[8,8,128]{2,1,0:T(8,128)S(1)}) custom-call(f32[5,8,8,128]{3,2,1,0:T(8,128)} %cons_hbm.1, f32[8,8,128]{2,1,0:T(8,128)} %sig_hbm.1), custom_call_target="tpu_custom_call" | custom-call | tf_op jit(solution)/shard_map/pallas_call | solution.py:551
  16.4 0.7 %shard_map.42 = (f32[5,8,8,128]{3,2,1,0:T(8,128)}, f32[8,8,128]{2,1,0:T(8,128)}) custom-call(f32[5,8,8,128]{3,2,1,0:T(8,128)S(1)} %get-tuple-element.4.adv, f32[8,8,128]{2,1,0:T(8,128)S(1)} %get-tuple-element.5.sig), custom_call_target="tpu_custom_call" | custom-call | tf_op jit(solution)/shard_map/pallas_call | solution.py:567

commit v5 on v4

--- a/solution.py
+++ b/solution.py
@@ -68,7 +68,7 @@
     ]
 
 
-def kernel(sizes, cons_hbm, sig_hbm, adv_ref, out_sig_ref, cons, sig, g0, g1, g2, g3, g4, t3, t4,
+def kernel(sizes, cons_hbm, sig_hbm, adv_ref, out_sig_ref, cons, sig, g0, g1, g2, g3, g4, t3, t4, sent,
            yas, zas, ybs, yrs, zrs, drs, x2s, y2s, z2s, d2s, in_sem, ready, send_sem, recv_sem):
     X, R, L = sig.shape
     H, D, DZ = R // 2, DEPTH, L // (4 * X)
@@ -92,7 +92,7 @@
 
         def copy(self, src, dst, offset):
             return pltpu.make_async_remote_copy(
-                src_ref=src, dst_ref=dst, send_sem=send_sem.at[self.n], recv_sem=recv_sem.at[self.n],
+                src_ref=src, dst_ref=dst, send_sem=send_sem, recv_sem=recv_sem.at[self.n],
                 device_id=device(offset), device_id_type=MESH)
 
         def send(self, src, offset, part=None):
@@ -109,15 +109,9 @@
                 self.copy(src, self.buf.at[at:self.used], offset).start()
             return at
 
-        def whole(self):
+        def arrived(self):
             assert self.used == self.buf.shape[0] and self.rows == self.spare.shape[0] * self.spare.shape[1]
-            return self.copy(self.spare, self.spare, NEAR[0])
-
-        def arrived(self):
-            self.whole().wait_recv()
-
-        def left(self):
-            self.whole().wait_send()
+            self.copy(self.spare, self.spare, NEAR[0]).wait_recv()
 
     groups = [Group(n, buf, size) for n, (buf, size) in enumerate(zip((g0, g1, g2, g3, g4), (g0, g1, g2, t3, t4)))]
     first, late, side, late_rho, second = groups
@@ -244,10 +238,8 @@
     for j, start, beyond in ((0, H, H - 1), (1, 0, H)):
         yrs[j, 0:X // 2] = pack_rows(state[0], start, H)
         yrs[j, X // 2:X // 2 + A] = pack_rows(state[0], beyond, 1)
-    yr, yb, xb, xe, xt = [], [], [], [], []
+    xb, xe, xt = [], [], []
     for j, d in ups:
-        yr.append(late.send(yrs.at[j], (0, d, 0)))
-        yb.append(late.send(ybs.at[j], (0, d, 0)))
         xb.append(late.send(cons.at[0:5, plane(d, 1)], (d, 0, 0)))
         xe.append(late.send(cons.at[4, plane(d)], (d, 0, 0)))
         xt.append(late.send(cons.at[0, planes(d, D - 1, 2)], (d, 0, 0)))
@@ -267,6 +259,10 @@
         dr[o] = late_rho.send(drs.at[n], o)
     zr_far = {}
     send_z(late_rho, zrs, Z_EDGE, zr_far)
+    yr, yb = [], []
+    for j, d in ups:
+        yr.append(late.send(yrs.at[j], (0, d, 0)))
+        yb.append(late.send(ybs.at[j], (0, d, 0)))
     side.arrived()
     send_z(late_rho, zrs, Z_VERTEX, zr_far)
 
@@ -488,44 +484,69 @@
     z, w = z_pairs(sig_of, 0, pack_planes(z_own, sx, outer), pack_planes(z_own, sy, every))
     q_own = roll(z_own, L // 2, 1)
     qz, qw = z_pairs(sig_of, 1, pack_planes(q_own, qx, outer), pack_planes(q_own, qy, range(-e, X + e)))
-    c, y = (cat(zero, sx[0:D], sigma1, sx[D:2 * D], zero), D + 1), (sy, D)
-    qc = cat(qx[0:D], source, qx[D:2 * D])
+    ghosts = [(z, w)]
     for sweep in range(1, SWEEPS):
-        last = sweep == SWEEPS - 1
-        ec, ey = D + 1 - sweep, 0 if last else D - sweep
-        cn, yy = around_planes(c, y, z, [(-ec, X + ec)])
-        yn = around_ghosts(y, [t[ec - ey:ec + X + ey] for t in yy], w, ey)
         zn, wn = around_packed(z, w)
-        cut = lambda v, have, e: v[have - e:have + X + e]
-        c = update(cut(qc, D, ec), [[cut(v, D, ec) for v in pair] for pair in coef_c], cn), ec
-        y = update(cut(qy, D - 1, ey), [[cut(v, D - 1, ey) for v in pair] for pair in coef_y], yn), ey
         z = [update(qz[j], coef_z[j], zn[j]) for j in range(2)]
-        if not last:
+        if sweep < SWEEPS - 1:
             w = [update(qw[j], coef_w[j], wn[j]) for j in range(2)]
-
-    own_planes = [(0, X)]
-    sigma4 = pick(c, own_planes)
-    out_sig_ref[...] = sigma4
-
-    def y_shift(step, by):
-        edge = row3 >= R - by if step == 1 else row3 < by
-        return jnp.where(edge, roll(y[0], -step * by, 1), roll(sigma4, -step * by, 1))
-
-    total = base[4] + middle * sigma4
-    for d in range(3):
-        if d == 0:
-            near_far = [[pick(c, own_planes, s * by) for by in (1, 2)] for s in (1, -1)]
-        elif d == 1:
-            near_far = [[y_shift(s, by) for by in (1, 2)] for s in (1, -1)]
-        else:
-            near_far = [[z_shift(sigma4, own_planes, z, s, by) for by in (1, 2)] for s in (1, -1)]
-        (p1, p2), (m1, m2) = near_far
-        adv_ref[1 + d] = base[1 + d] + ((-4.0 * STEP_DT / 6.0) * (p1 - m1) + (0.5 * STEP_DT / 6.0) * (p2 - m2))
-        a = part[d]
-        total = total + (a[0] * m2 + a[1] * m1 + a[3] * p1 + a[4] * p2)
-    adv_ref[4] = total
-    for group in groups:
-        group.left()
+        ghosts.append((z, w))
+
+    def lane_ghost(sweep, which, p):
+        return sweep, which, p
+
+    def one_shift(tile, ghost, step, by=1):
+        sweep, which, p = ghost
+        pair = ghosts[sweep][which]
+        if step == 1:
+            return jnp.where(lane2 >= L - by, roll(pair[1], L - by - wide * p, 1), roll(tile, -by, 1))
+        return jnp.where(lane2 < by, roll(pair[0], by - wide * p, 1), roll(tile, by, 1))
+
+    tiles = lambda value, lo: {lo + k: value[k] for k in range(value.shape[0])}
+    c = {**tiles(sigma1, 0), **tiles(sx[0:D], -D), **tiles(sx[D:2 * D], X), -D - 1: zero[0], X + D: zero[0]}
+    qc = {**tiles(source, 0), **tiles(qx[0:D], -D), **tiles(qx[D:2 * D], X)}
+    y, qy = tiles(sy, -D), tiles(qy, -e)
+    cs, ys = [c] + [{} for _ in range(1, SWEEPS)], [y] + [{} for _ in range(1, SWEEPS)]
+
+    def sweep_plane(sweep, p):
+        c, y = cs[sweep - 1], ys[sweep - 1]
+        ec, ey = D + 1 - sweep, 0 if sweep == SWEEPS - 1 else D - sweep
+        if not -ec <= p < X + ec:
+            return
+        cy = [ring(c[p], y[p], s, 0) for s in (1, -1)]
+        ghost = lane_ghost(sweep - 1, 0, p)
+        nbr = [(c[p + 1], c[p - 1]), [t[0] for t in cy], [one_shift(c[p], ghost, s) for s in (1, -1)]]
+        cs[sweep][p] = update(qc[p], [[v[D + p] for v in pair] for pair in coef_c], nbr)
+        if -ey <= p < X + ey:
+            ghost = lane_ghost(sweep - 1, 1, p)
+            nbr = [(y[p + 1], y[p - 1]), [t[1] for t in cy], [one_shift(y[p], ghost, s) for s in (1, -1)]]
+            ys[sweep][p] = update(qy[p], [[v[e + p] for v in pair] for pair in coef_y], nbr)
+
+    def flux_plane(p):
+        if not 0 <= p < X:
+            return
+        c, y, ghost = cs[SWEEPS - 1], ys[SWEEPS - 1], lane_ghost(SWEEPS - 1, 0, p)
+        out_sig_ref[p] = c[p]
+
+        def y_shift(step, by):
+            edge = row2 >= R - by if step == 1 else row2 < by
+            return jnp.where(edge, roll(y[p], -step * by, 0), roll(c[p], -step * by, 0))
+
+        total = base[4][p] + middle[p] * c[p]
+        shifts = [lambda s, by: c[p + s * by], y_shift, lambda s, by: one_shift(c[p], ghost, s, by)]
+        for d in range(3):
+            (p1, p2), (m1, m2) = [[shifts[d](s, by) for by in (1, 2)] for s in (1, -1)]
+            adv_ref[1 + d, p] = base[1 + d][p] + ((-4.0 * STEP_DT / 6.0) * (p1 - m1) + (0.5 * STEP_DT / 6.0) * (p2 - m2))
+            a = [v[p] for v in part[d]]
+            total = total + (a[0] * m2 + a[1] * m1 + a[3] * p1 + a[4] * p2)
+        adv_ref[4, p] = total
+
+    for step in range(-D, X + D + 2 * SWEEPS):
+        for sweep in range(1, SWEEPS):
+            sweep_plane(sweep, step - 2 * (sweep - 1))
+        flux_plane(step - 2 * (SWEEPS - 1) - 1)
+    assert sum(group.rows for group in groups) == sent.shape[0]
+    second.copy(sent, sent, NEAR[0]).wait_send()
 
 
 def write(adv, sig, adv_hbm, sig_hbm, sem):
@@ -547,7 +568,8 @@
         vm = lambda *shape: pltpu.VMEM((*shape, R, L), f32)
         nd = len(XY_MOVES)
         tiles = landing(X, R, sizes)
-        spare = [pltpu.VMEM((R * n + sum(part), 1, L), f32) for n, part in tiles[3:]]
+        rows = [R * n + sum(part) for n, part in tiles]
+        spare = [pltpu.VMEM((n, 1, L), f32) for n in (rows[3], rows[4], sum(rows))]
         outs = pl.pallas_call(
             functools.partial(kernel, sizes),
             out_shape=(pltpu.VMEM(conserved.shape, f32), pltpu.VMEM(sigma_guess.shape, f32)),
@@ -559,7 +581,7 @@
                 vm(2, 2 * D), vm(2, 2 * H), vm(), vm(nd, 2),
                 pltpu.SemaphoreType.DMA((2,)),
                 pltpu.SemaphoreType.REGULAR,
-                pltpu.SemaphoreType.DMA((len(tiles),)),
+                pltpu.SemaphoreType.DMA,
                 pltpu.SemaphoreType.DMA((len(tiles),)),
             ],
             compiler_params=pltpu.CompilerParams(collective_id=0, has_side_effects=True),

time: 17.2 us -> 16.9 us (0.983)
  Pallas kernels: 16.5 us -> 16.1 us
    pallas_call x1, Pallas kernels: 15.8 us -> 15.4 us  [on_device(): pl.pallas_call(functools.partial(kernel, sizes), out_shape=(pltpu.VMEM(co...]
where the time goes in v5:
time: 16.9 us; the launch traced here: 16.7 us
  Pallas kernels  16.1 us (95%)
  between operations  0.64 us (4%)
    pallas_call x1, Pallas kernels, on_device(): pl.pallas_call(functools.partial(kernel, sizes), out_shape=(pltpu.VMEM(co...  15.4 us
    pallas_call x1, Pallas kernels, on_device(): pl.pallas_call(write, out_shape=tuple((jax.ShapeDtypeStruct(a.shape, f32)...  0.69 us

profile of v5, /device:TPU:0, one launch (start us, length us, event | category | flops | bytes accessed | tf_op | source)
XLA Modules:
  0.0 16.7 jit_solution(9313070096835227326)
XLA Ops:
  0.6 15.4 %shard_map.41 = (f32[5,8,8,128]{3,2,1,0:T(8,128)S(1)}, f32[8,8,128]{2,1,0:T(8,128)S(1)}) custom-call(f32[5,8,8,128]{3,2,1,0:T(8,128)} %cons_hbm.1, f32[8,8,128]{2,1,0:T(8,128)} %sig_hbm.1), custom_call_target="tpu_custom_call" | custom-call | tf_op jit(solution)/shard_map/pallas_call | solution.py:573
  16.0 0.7 %shard_map.42 = (f32[5,8,8,128]{3,2,1,0:T(8,128)}, f32[8,8,128]{2,1,0:T(8,128)}) custom-call(f32[5,8,8,128]{3,2,1,0:T(8,128)S(1)} %get-tuple-element.4.adv, f32[8,8,128]{2,1,0:T(8,128)S(1)} %get-tuple-element.5.sig), custom_call_target="tpu_custom_call" | custom-call | tf_op jit(solution)/shard_map/pallas_call | solution.py:589

commit v6 on v5

--- a/solution.py
+++ b/solution.py
@@ -61,9 +61,9 @@
     near, corner = len(sent(Z_NEAR)), 2 * len(XY_MOVES)
     return [
         (2 * (5 * A + 5 + 2), []),
-        (2 * (H + A + 4 * B + 5 + 1 + DEPTH - 1), []),
+        (2 * (H + 3 * A + B + 5 + 1 + DEPTH - 1), []),
         (near, []),
-        (corner + full, part),
+        (len(XY_MOVES) + full, part + [2] * len(XY_MOVES)),
         (corner + near + full + 2 * 2 * H + 2 * 2 * DEPTH, part),
     ]
 
@@ -128,10 +128,10 @@
             out = jnp.where((r + (2 * R - first - n * g)) % R < n, part, out)
         return out
 
-    def unpack_rows(after, before, n, reach=0):
+    def unpack_rows(after, before, n):
         low = rows(after.shape) < H
         return jnp.concatenate(
-            [jnp.where(low, roll(after, -n * g - reach, 1), roll(before, reach - n * g, 1)) for g in range(R // n)],
+            [jnp.where(low, roll(after, -n * g, 1), roll(before, -n * g, 1)) for g in range(R // n)],
             axis=0)
 
     lane2, row2 = lanes((R, L)), rows((R, L))
@@ -231,13 +231,11 @@
     for o in NEAR:
         pl.semaphore_signal(ready, inc=1, device_id=device(o), device_id_type=MESH)
 
-    for f in range(4):
-        field = state[1 + f] if f < 3 else energy
-        ybs[0, f * B:(f + 1) * B] = pack_rows(field, R - 2, 2)
-        ybs[1, f * B:(f + 1) * B] = pack_rows(field, 0, 2)
-    for j, start, beyond in ((0, H, H - 1), (1, 0, H)):
-        yrs[j, 0:X // 2] = pack_rows(state[0], start, H)
-        yrs[j, X // 2:X // 2 + A] = pack_rows(state[0], beyond, 1)
+    for j, second_row, start in ((0, R - 2, R - 1 - H), (1, 1, 1)):
+        for f in range(3):
+            ybs[j, f * A:(f + 1) * A] = pack_rows(state[1 + f], second_row, 1)
+        ybs[j, 3 * A:3 * A + B] = pack_rows(energy, (R - 2, 0)[j], 2)
+        yrs[j] = pack_rows(state[0], start, H)
     xb, xe, xt = [], [], []
     for j, d in ups:
         xb.append(late.send(cons.at[0:5, plane(d, 1)], (d, 0, 0)))
@@ -256,7 +254,8 @@
     send_z(side, zrs, Z_NEAR, zr)
     side_slots = dict(zr)
     for n, o in enumerate(XY_MOVES):
-        dr[o] = late_rho.send(drs.at[n], o)
+        dr[o] = late_rho.send(drs.at[n, 0], o)
+        late_rho.send(drs.at[n, 1], o, slice(0, 2) if o[1] == 1 else slice(R - 2, R))
     zr_far = {}
     send_z(late_rho, zrs, Z_EDGE, zr_far)
     yr, yb = [], []
@@ -345,12 +344,21 @@
 
     late.arrived()
     core = state[0:4] + [energy]
-    rho_y = unpack_rows(g1[yr[1]:yr[1] + X // 2], g1[yr[0]:yr[0] + X // 2], H)
-    rho_yy = unpack_rows(g1[yr[1] + X // 2:yr[1] + X // 2 + A], g1[yr[0] + X // 2:yr[0] + X // 2 + A], 1, 1)
+    near_row = (row3 == 0) | (row3 == R - 1)
+
+    def first_rows(f):
+        return unpack_rows(g0[ya[1] + f * A:ya[1] + (f + 1) * A], g0[ya[0] + f * A:ya[0] + (f + 1) * A], 1)
+
+    def late_rows(at, to, n):
+        return unpack_rows(g1[yb[1] + at:yb[1] + to], g1[yb[0] + at:yb[0] + to], n)
+
+    rho_before, rho_after = [cat(*[roll(g1[yr[j]:yr[j] + X // 2], -H * k, 1) for k in range(R // H)]) for j in range(2)]
+    rho_y = jnp.where(near_row, first_rows(0), jnp.where(row3 < H, rho_after, rho_before))
+    rho_yy = jnp.where(row3 < H, roll(rho_after, -1, 1), roll(rho_before, 1, 1))
     xn = [[g0[xa[j] + f][None] for f in range(4)] + [g1[xe[j]][None]] for j in range(2)]
     xc = [cat(g1[xb[0] + f][None], xn[0][f], core[f], xn[1][f], g1[xb[1] + f][None]) for f in range(5)]
-    yc = [rho_y] + [unpack_rows(g1[yb[1] + f * B:yb[1] + (f + 1) * B], g1[yb[0] + f * B:yb[0] + (f + 1) * B], 2)
-                    for f in range(4)]
+    yc = [rho_y] + [jnp.where(near_row, first_rows(1 + f), late_rows(f * A, (f + 1) * A, 1)) for f in range(3)]
+    yc.append(late_rows(3 * A, 3 * A + B, 2))
     zc = [cat(*[roll(zmerged[f // 4], -4 * (f * X + p), 1)[None] for p in range(X)]) for f in range(4)]
     zc.append(cat(*[roll(zmerged[1], -4 * (X + p), 1)[None] for p in range(X)]))
 
@@ -577,7 +585,7 @@
             out_specs=(pl.BlockSpec(memory_space=pltpu.VMEM),) * 2,
             scratch_shapes=[
                 vm(5, X), vm(X), *[vm(n + len(part)) for n, part in tiles], *spare,
-                vm(2, 5 * A), vm(2), vm(2, 4 * B), vm(2, H + A), vm(), vm(nd, 2),
+                vm(2, 5 * A), vm(2), vm(2, 3 * A + B), vm(2, H), vm(), vm(nd, 2),
                 vm(2, 2 * D), vm(2, 2 * H), vm(), vm(nd, 2),
                 pltpu.SemaphoreType.DMA((2,)),
                 pltpu.SemaphoreType.REGULAR,

time: 16.9 us -> 16.9 us (level)
  no operation moved by 1% of the time
where the time goes in v6:
time: 16.9 us; the launch traced here: 16.7 us
  Pallas kernels  16 us (95%)
  between operations  0.64 us (4%)
    pallas_call x1, Pallas kernels, on_device(): pl.pallas_call(functools.partial(kernel, sizes), out_shape=(pltpu.VMEM(co...  15.4 us
    pallas_call x1, Pallas kernels, on_device(): pl.pallas_call(write, out_shape=tuple((jax.ShapeDtypeStruct(a.shape, f32)...  0.69 us

profile of v6, /device:TPU:0, one launch (start us, length us, event | category | flops | bytes accessed | tf_op | source)
XLA Modules:
  0.0 16.7 jit_solution(5726240603111006169)
XLA Ops:
  0.6 15.4 %shard_map.41 = (f32[5,8,8,128]{3,2,1,0:T(8,128)S(1)}, f32[8,8,128]{2,1,0:T(8,128)S(1)}) custom-call(f32[5,8,8,128]{3,2,1,0:T(8,128)} %cons_hbm.1, f32[8,8,128]{2,1,0:T(8,128)} %sig_hbm.1), custom_call_target="tpu_custom_call" | custom-call | tf_op jit(solution)/shard_map/pallas_call | solution.py:581
  16.0 0.7 %shard_map.42 = (f32[5,8,8,128]{3,2,1,0:T(8,128)}, f32[8,8,128]{2,1,0:T(8,128)}) custom-call(f32[5,8,8,128]{3,2,1,0:T(8,128)S(1)} %get-tuple-element.4.adv, f32[8,8,128]{2,1,0:T(8,128)S(1)} %get-tuple-element.5.sig), custom_call_target="tpu_custom_call" | custom-call | tf_op jit(solution)/shard_map/pallas_call | solution.py:597

commit v7 on v6

--- a/solution.py
+++ b/solution.py
@@ -60,15 +60,16 @@
     A, B, H = X // R, 2 * X // R, X // 2
     near, corner = len(sent(Z_NEAR)), 2 * len(XY_MOVES)
     return [
-        (2 * (5 * A + 5 + 2), []),
+        (2 * (5 + 2), []),
         (2 * (H + 3 * A + B + 5 + 1 + DEPTH - 1), []),
         (near, []),
         (len(XY_MOVES) + full, part + [2] * len(XY_MOVES)),
         (corner + near + full + 2 * 2 * H + 2 * 2 * DEPTH, part),
+        (2 * 5 * A, []),
     ]
 
 
-def kernel(sizes, cons_hbm, sig_hbm, adv_ref, out_sig_ref, cons, sig, g0, g1, g2, g3, g4, t3, t4, sent,
+def kernel(sizes, cons_hbm, sig_hbm, adv_ref, out_sig_ref, cons, sig, g0, g1, g2, g3, g4, g5, t3, t4, sent,
            yas, zas, ybs, yrs, zrs, drs, x2s, y2s, z2s, d2s, in_sem, ready, send_sem, recv_sem):
     X, R, L = sig.shape
     H, D, DZ = R // 2, DEPTH, L // (4 * X)
@@ -113,8 +114,9 @@
             assert self.used == self.buf.shape[0] and self.rows == self.spare.shape[0] * self.spare.shape[1]
             self.copy(self.spare, self.spare, NEAR[0]).wait_recv()
 
-    groups = [Group(n, buf, size) for n, (buf, size) in enumerate(zip((g0, g1, g2, g3, g4), (g0, g1, g2, t3, t4)))]
-    first, late, side, late_rho, second = groups
+    groups = [Group(n, buf, size)
+              for n, (buf, size) in enumerate(zip((g0, g1, g2, g3, g4, g5), (g0, g1, g2, t3, t4, g5)))]
+    first, late, side, late_rho, second, first_y = groups
 
     rows = lambda shape: iota(shape, len(shape) - 2)
     lanes = lambda shape: iota(shape, len(shape) - 1)
@@ -222,7 +224,7 @@
     zas[0] = pack_lanes(state[0:4], 4)
     zas[1] = pack_lanes([state[4], energy], 4)
     pl.semaphore_wait(barrier, len(NEAR))
-    ya = [first.send(yas.at[j], (0, d, 0)) for j, d in ups]
+    ya = [first_y.send(yas.at[j], (0, d, 0)) for j, d in ups]
     xa = []
     for j, d in ups:
         xa.append(first.send(cons.at[0:4, plane(d)], (d, 0, 0)))
@@ -262,43 +264,20 @@
     for j, d in ups:
         yr.append(late.send(yrs.at[j], (0, d, 0)))
         yb.append(late.send(ybs.at[j], (0, d, 0)))
-    side.arrived()
-    send_z(late_rho, zrs, Z_VERTEX, zr_far)
 
     inv0 = 1.0 / state[0]
     fields = [inv0] + [state[k] * inv0 for k in (1, 2, 3)] + [state[4]]
     own = [[[roll(v, -s, axis) for s in (1, -1)] for axis in (1, 2)] for v in fields]
     region = ((lane2 + 2) % L) // (4 * X)
 
-    first.arrived()
-
     def to_speed(t):
         r = 1.0 / t[0]
         return [r] + [m * r for m in t[1:4]] + [t[4]]
 
-    xg = [to_speed([g0[xa[j] + f] for f in range(5)]) for j in range(2)]
-    yg = [to_speed([g0[ya[j] + f * A:ya[j] + (f + 1) * A] for f in range(5)]) for j in range(2)]
-    zmerged = [jnp.where(lane2 % 4 < 2, g0[za[1] + v], g0[za[0] + v]) for v in range(2)]
-    zinv = 1.0 / jnp.where(region == 0, zmerged[0], 1.0)
-    shifted = [roll(zinv, 4 * X * k, 1) for k in (1, 2, 3)]
-    zspeed = zmerged[0] * jnp.where(region == 1, shifted[0], jnp.where(region == 2, shifted[1], shifted[2]))
-    zspeed = jnp.where(region == 0, zinv, zspeed)
-
-    def neighbours(f):
-        v, ((yp, ym), (zp, zm)) = fields[f], own[f]
-        after = cat(*[roll(yg[1][f], R - 1 - p, 1) for p in range(R)])
-        before = cat(*[roll(yg[0][f], 1 - p, 1) for p in range(R)])
-        t, k = (zspeed, f * X) if f < 4 else (zmerged[1], 0)
-        high = cat(*[roll(t, L - 1 - 4 * (k + p), 1)[None] for p in range(X)])
-        low = cat(*[roll(t, 1 - 4 * (k + p), 1)[None] for p in range(X)])
-        return [(cat(v[1:X], xg[1][f][None]), cat(xg[0][f][None], v[0:X - 1])),
-                (jnp.where(row3 == R - 1, after, yp), jnp.where(row3 == 0, before, ym)),
-                (jnp.where(lane3 == L - 1, high, zp), jnp.where(lane3 == 0, low, zm))]
-
     def coefficients(inv_m, inv_n):
         ws = [[inv_m + inv_n[d][s] for s in range(2)] for d in range(3)]
         scale = ALPHA / (2.0 * inv_m + ALPHA * sum(w for pair in ws for w in pair))
-        return [[w * scale for w in pair] for pair in ws], scale
+        return [[w * scale for w in pair] for pair in ws]
 
     def update(source, ws, nbr):
         acc = source
@@ -307,16 +286,50 @@
                 acc = acc + ws[d][s] * nbr[d][s]
         return acc
 
-    near_w, near_scale = coefficients(inv0, neighbours(0))
-    g = []
-    for k in (1, 2, 3):
-        n = neighbours(k)
-        g.append([n[d][0] - n[d][1] for d in range(3)])
-    div = g[0][0] + g[1][1] + g[2][2]
-    source = (g[0][0] * g[0][0] + g[1][1] * g[1][1] + g[2][2] * g[2][2]
-              + 2.0 * (g[0][1] * g[1][0] + g[0][2] * g[2][0] + g[1][2] * g[2][1]) + div * div)
+    first.arrived()
+    xg = [to_speed([g0[xa[j] + f] for f in range(5)]) for j in range(2)]
+    zmerged = [jnp.where(lane2 % 4 < 2, g0[za[1] + v], g0[za[0] + v]) for v in range(2)]
+    zinv = 1.0 / jnp.where(region == 0, zmerged[0], 1.0)
+    shifted = [roll(zinv, 4 * X * k, 1) for k in (1, 2, 3)]
+    zspeed = zmerged[0] * jnp.where(region == 1, shifted[0], jnp.where(region == 2, shifted[1], shifted[2]))
+    zspeed = jnp.where(region == 0, zinv, zspeed)
+
+    def xz_neighbours(f):
+        v, (_, (zp, zm)) = fields[f], own[f]
+        t, k = (zspeed, f * X) if f < 4 else (zmerged[1], 0)
+        high = cat(*[roll(t, L - 1 - 4 * (k + p), 1)[None] for p in range(X)])
+        low = cat(*[roll(t, 1 - 4 * (k + p), 1)[None] for p in range(X)])
+        return [(cat(v[1:X], xg[1][f][None]), cat(xg[0][f][None], v[0:X - 1])),
+                (jnp.where(lane3 == L - 1, high, zp), jnp.where(lane3 == 0, low, zm))]
+
+    ws = [None] * 3
+    ws[0], ws[2] = [[inv0 + v for v in pair] for pair in xz_neighbours(0)]
+    (g00, g02), (g10, g12), (g20, g22) = [[p - m for p, m in xz_neighbours(k)] for k in (1, 2, 3)]
+    squares, div = g00 * g00 + g22 * g22 + 2.0 * (g02 * g20), g00 + g22
+    weight = ws[0][0] + ws[0][1] + ws[2][0] + ws[2][1]
+    (xp, xm), (zp, zm) = xz_neighbours(4)
+    inflow = ws[0][0] * xp + ws[0][1] * xm + ws[2][0] * zp + ws[2][1] * zm
+
+    side.arrived()
+    send_z(late_rho, zrs, Z_VERTEX, zr_far)
+    first_y.arrived()
+    yg = [to_speed([g5[ya[j] + f * A:ya[j] + (f + 1) * A] for f in range(5)]) for j in range(2)]
+
+    def y_neighbours(f):
+        yp, ym = own[f][0]
+        after = cat(*[roll(yg[1][f], R - 1 - p, 1) for p in range(R)])
+        before = cat(*[roll(yg[0][f], 1 - p, 1) for p in range(R)])
+        return jnp.where(row3 == R - 1, after, yp), jnp.where(row3 == 0, before, ym)
+
+    ws[1] = [inv0 + v for v in y_neighbours(0)]
+    near_scale = ALPHA / (2.0 * inv0 + ALPHA * (weight + ws[1][0] + ws[1][1]))
+    g01, g11, g21 = [p - m for p, m in (y_neighbours(k) for k in (1, 2, 3))]
+    div = div + g11
+    source = squares + g11 * g11 + 2.0 * (g01 * g10 + g12 * g21) + div * div
     source = source * (0.5 * near_scale)
-    sigma1 = update(source, near_w, neighbours(4))
+    yp, ym = y_neighbours(4)
+    sigma1 = source + near_scale * (inflow + ws[1][0] * yp + ws[1][1] * ym)
+    near_w = [[w * near_scale for w in pair] for pair in ws]
 
     z_fold = jnp.where(lane3 == DZ - 1, near_w[2][0] * roll(sigma1, -1, 2),
                        jnp.where(lane3 == L - DZ, near_w[2][1] * roll(sigma1, 1, 2), 0.0))
@@ -347,7 +360,7 @@
     near_row = (row3 == 0) | (row3 == R - 1)
 
     def first_rows(f):
-        return unpack_rows(g0[ya[1] + f * A:ya[1] + (f + 1) * A], g0[ya[0] + f * A:ya[0] + (f + 1) * A], 1)
+        return unpack_rows(g5[ya[1] + f * A:ya[1] + (f + 1) * A], g5[ya[0] + f * A:ya[0] + (f + 1) * A], 1)
 
     def late_rows(at, to, n):
         return unpack_rows(g1[yb[1] + at:yb[1] + to], g1[yb[0] + at:yb[0] + to], n)
@@ -461,7 +474,7 @@
     inv_z, inv_w = [1.0 / t for t in rho_z], [1.0 / t for t in rho_w]
     beyond = [1.0 / z_side(rho_of, 0, dz, 1) for dz in (-1, 1)]
     far_coef = coefficients(pick(inv_c, [(-D, 0), (X, X + D)]),
-                            around_planes(inv_c, inv_y, inv_z, [(-D, 0), (X, X + D)])[0])[0]
+                            around_planes(inv_c, inv_y, inv_z, [(-D, 0), (X, X + D)])[0])
     coef_c = [[cat(far[0:D], mine, far[D:2 * D]) for far, mine in zip(*pair)] for pair in zip(far_coef, near_w)]
     e = D - 1
     rim = jnp.zeros((e, R, L), jnp.float32)
@@ -469,7 +482,7 @@
     inv_yy = cat(rim, 1.0 / rho_yy, rim)
     row = rows(inv_yy.shape)
     yy = [jnp.where(row == at, inv_yy, t) for t, at in zip(yy, (H - 1, H))]
-    coef_y = coefficients(pick(inv_y, [(-e, X + e)]), around_ghosts(inv_y, yy, inv_w, e))[0]
+    coef_y = coefficients(pick(inv_y, [(-e, X + e)]), around_ghosts(inv_y, yy, inv_w, e))
     coef_y[1] = [jnp.where(row == at, 0.0, t) for t, at in zip(coef_y[1], (H - 1, H))]
     zn, wn = around_packed(inv_z, inv_w)
     coef_z, coef_w = [], []
@@ -477,10 +490,9 @@
         last = lane2 % wide == at
         pair = list(zn[j][2])
         pair[1 - j] = jnp.where(last, beyond[j], pair[1 - j])
-        ws = coefficients(inv_z[j], [*zn[j][0:2], pair])[0]
-        ws[2][1 - j] = jnp.where(last, 0.0, ws[2][1 - j])
-        coef_z.append(ws)
-        coef_w.append(coefficients(inv_w[j], wn[j])[0])
+        coef_z.append(coefficients(inv_z[j], [*zn[j][0:2], pair]))
+        coef_z[j][2][1 - j] = jnp.where(last, 0.0, coef_z[j][2][1 - j])
+        coef_w.append(coefficients(inv_w[j], wn[j]))
 
     second.arrived()
     zero = jnp.zeros((1, R, L), jnp.float32)

time: 16.9 us -> 16.7 us (0.988)
  Pallas kernels: 16 us -> 15.8 us
    pallas_call x1, Pallas kernels: 15.4 us -> 15.1 us  [on_device(): pl.pallas_call(functools.partial(kernel, sizes), out_shape=(pltpu.VMEM(co...]
where the time goes in v7:
time: 16.7 us; the launch traced here: 16.5 us
  Pallas kernels  15.8 us (95%)
  between operations  0.64 us (4%)
    pallas_call x1, Pallas kernels, on_device(): pl.pallas_call(functools.partial(kernel, sizes), out_shape=(pltpu.VMEM(co...  15.1 us
    pallas_call x1, Pallas kernels, on_device(): pl.pallas_call(write, out_shape=tuple((jax.ShapeDtypeStruct(a.shape, f32)...  0.69 us

profile of v7, /device:TPU:0, one launch (start us, length us, event | category | flops | bytes accessed | tf_op | source)
XLA Modules:
  0.0 16.5 jit_solution(14133982843358546826)
XLA Ops:
  0.6 15.1 %shard_map.41 = (f32[5,8,8,128]{3,2,1,0:T(8,128)S(1)}, f32[8,8,128]{2,1,0:T(8,128)S(1)}) custom-call(f32[5,8,8,128]{3,2,1,0:T(8,128)} %cons_hbm.1, f32[8,8,128]{2,1,0:T(8,128)} %sig_hbm.1), custom_call_target="tpu_custom_call" | custom-call | tf_op jit(solution)/shard_map/pallas_call | solution.py:593
  15.8 0.7 %shard_map.42 = (f32[5,8,8,128]{3,2,1,0:T(8,128)}, f32[8,8,128]{2,1,0:T(8,128)}) custom-call(f32[5,8,8,128]{3,2,1,0:T(8,128)S(1)} %get-tuple-element.4.adv, f32[8,8,128]{2,1,0:T(8,128)S(1)} %get-tuple-element.5.sig), custom_call_target="tpu_custom_call" | custom-call | tf_op jit(solution)/shard_map/pallas_call | solution.py:609

commit v8 on v7

--- a/solution.py
+++ b/solution.py
@@ -238,11 +238,6 @@
             ybs[j, f * A:(f + 1) * A] = pack_rows(state[1 + f], second_row, 1)
         ybs[j, 3 * A:3 * A + B] = pack_rows(energy, (R - 2, 0)[j], 2)
         yrs[j] = pack_rows(state[0], start, H)
-    xb, xe, xt = [], [], []
-    for j, d in ups:
-        xb.append(late.send(cons.at[0:5, plane(d, 1)], (d, 0, 0)))
-        xe.append(late.send(cons.at[4, plane(d)], (d, 0, 0)))
-        xt.append(late.send(cons.at[0, planes(d, D - 1, 2)], (d, 0, 0)))
     lane3 = lanes(energy.shape)
     row3 = rows(energy.shape)
     rho_zz = jnp.where(lane3 == DZ - 1, roll(state[0], -1, 2), roll(state[0], 1, 2))
@@ -260,6 +255,11 @@
         late_rho.send(drs.at[n, 1], o, slice(0, 2) if o[1] == 1 else slice(R - 2, R))
     zr_far = {}
     send_z(late_rho, zrs, Z_EDGE, zr_far)
+    xb, xe, xt = [], [], []
+    for j, d in ups:
+        xb.append(late.send(cons.at[0:5, plane(d, 1)], (d, 0, 0)))
+        xe.append(late.send(cons.at[4, plane(d)], (d, 0, 0)))
+        xt.append(late.send(cons.at[0, planes(d, D - 1, 2)], (d, 0, 0)))
     yr, yb = [], []
     for j, d in ups:
         yr.append(late.send(yrs.at[j], (0, d, 0)))

time: 16.7 us -> 16.7 us (level)
  no operation moved by 1% of the time
where the time goes in v8:
time: 16.7 us; the launch traced here: 16.5 us
  Pallas kernels  15.8 us (95%)
  between operations  0.64 us (4%)
    pallas_call x1, Pallas kernels, on_device(): pl.pallas_call(functools.partial(kernel, sizes), out_shape=(pltpu.VMEM(co...  15.1 us
    pallas_call x1, Pallas kernels, on_device(): pl.pallas_call(write, out_shape=tuple((jax.ShapeDtypeStruct(a.shape, f32)...  0.69 us

profile of v8, /device:TPU:0, one launch (start us, length us, event | category | flops | bytes accessed | tf_op | source)
XLA Modules:
  0.0 16.5 jit_solution(344064330527739680)
XLA Ops:
  0.6 15.1 %shard_map.41 = (f32[5,8,8,128]{3,2,1,0:T(8,128)S(1)}, f32[8,8,128]{2,1,0:T(8,128)S(1)}) custom-call(f32[5,8,8,128]{3,2,1,0:T(8,128)} %cons_hbm.1, f32[8,8,128]{2,1,0:T(8,128)} %sig_hbm.1), custom_call_target="tpu_custom_call" | custom-call | tf_op jit(solution)/shard_map/pallas_call | solution.py:593
  15.8 0.7 %shard_map.42 = (f32[5,8,8,128]{3,2,1,0:T(8,128)}, f32[8,8,128]{2,1,0:T(8,128)}) custom-call(f32[5,8,8,128]{3,2,1,0:T(8,128)S(1)} %get-tuple-element.4.adv, f32[8,8,128]{2,1,0:T(8,128)S(1)} %get-tuple-element.5.sig), custom_call_target="tpu_custom_call" | custom-call | tf_op jit(solution)/shard_map/pallas_call | solution.py:609
